TPU v7x, 128 devices: a whole 4x4x4 slice. The times are simulated.
128 devices in a mesh: head: 8 (over z_lo, x), blk: 16 (over z_hi, y, core).
Axes of the slice: x: 4, y: 4, z: 4 (z_hi: 2, z_lo: 2; z = z_hi * 2 + z_lo), core: 2. Of those that a mesh axis runs over, the one named last changes fastest.
Arguments:
- hidden_in: bfloat16 [8192, 4096], P(('blk', 'head')), may hold values from -6 to 6
- queries: bfloat16 [8192, 2048], P(('blk', 'head')), may hold values from -26 to 26
- key_states: bfloat16 [8192, 1024], P(('blk', 'head')), may hold values from -5 to 5
- value_states: bfloat16 [8192, 1024], P(('blk', 'head')), may hold values from -6 to 6
- out_weight: bfloat16 [2048, 4096], P('head'), may hold values from -0.125 to 0.125
- norm_gain: float32 [4096], replicated, may hold values from 0.1 to 1.9
- gate_weight: bfloat16 [4096, 7168], P(None, 'head'), may hold values from -0.09375 to 0.09375
- up_weight: bfloat16 [4096, 7168], P(None, 'head'), may hold values from -0.09375 to 0.09375
- down_weight: bfloat16 [7168, 4096], P('head'), may hold values from -0.0625 to 0.0625
Outputs:
- layer_out: bfloat16 [8192, 4096], P(('blk', 'head'))
All inputs are finite; a program needn't handle non-finite values.
Results may differ from a plain program's by a relative error of at most 0.018.
Values may be sent and summed in bfloat16 or wider, within the bound.
A program may use at most 192 MiB of HBM per device.

v0:
```python
import jax
import jax.numpy as jnp
from jax import lax
from jax.sharding import PartitionSpec as P

HEADS = 16
KV_HEADS = 8
HEAD_DIM = 128


negative_fill = -1e30


def sent_together(arrays, axis, dim, along):
    ends, at = ([], 0)
    for a in arrays[:-1]:
        at += a.shape[along]
        ends.append(at)
    both = jnp.concatenate(arrays, axis=along)
    return tuple(jnp.split(lax.all_gather(both, axis, axis=dim, tiled=True), ends, axis=along))


def absorb_rows(running, query_groups, query_pos, key_block, value_block, key_pos):
    row_peak, row_total, weighted = running
    key_count = key_block.shape[0]
    group_count = query_groups.shape[1]
    head_size = query_groups.shape[3]
    key_heads = key_block.reshape(key_count, group_count, head_size)
    value_heads = value_block.reshape(key_count, group_count, head_size)
    scores = jnp.einsum(
        "qgrd,kgd->grqk", query_groups, key_heads, preferred_element_type=jnp.float32
    ) * head_size ** (-0.5)
    visible = key_pos[None, :] <= query_pos[:, None]
    new_peak = jnp.maximum(row_peak, jnp.max(jnp.where(visible, scores, negative_fill), axis=-1))
    exp_scores = jnp.where(visible, jnp.exp(scores - new_peak[..., None]), 0.0)
    new_total = jnp.sum(exp_scores, axis=-1)
    products = jnp.einsum(
        "grqk,kgd->grqd",
        exp_scores.astype(jnp.bfloat16),
        value_heads,
        preferred_element_type=jnp.float32,
    )
    return (new_peak, new_total, products)


def local(
    hidden_in,
    queries,
    key_states,
    value_states,
    out_weight,
    norm_gain,
    gate_weight,
    up_weight,
    down_weight,
):
    own_block = lax.axis_index("blk")
    query_local, key_local, value_local = (
        lax.all_to_all(queries, "head", split_axis=1, concat_axis=0, tiled=True),
        lax.all_to_all(key_states, "head", split_axis=1, concat_axis=0, tiled=True),
        lax.all_to_all(value_states, "head", split_axis=1, concat_axis=0, tiled=True),
    )
    block_rows = query_local.shape[0]
    query_width = query_local.shape[1]
    key_width = key_local.shape[1]
    group_count = key_width // HEAD_DIM
    group_ratio = HEADS // KV_HEADS
    local_index = jnp.arange(block_rows, dtype=jnp.int32)
    start_state = (
        jnp.full((group_count, group_ratio, block_rows), negative_fill, jnp.float32),
        jnp.zeros((group_count, group_ratio, block_rows), jnp.float32),
        jnp.zeros((group_count, group_ratio, block_rows, HEAD_DIM), jnp.float32),
    )
    query_pos = own_block * block_rows + local_index
    query_groups = query_local.reshape(block_rows, group_count, group_ratio, HEAD_DIM)
    last_query = own_block * block_rows + block_rows - 1
    key_block, value_block = sent_together((key_local, value_local), "blk", 0, 1)
    key_pos = jnp.arange(key_block.shape[0], dtype=jnp.int32)

    def skipped(state):
        return state

    def worked(state):
        return absorb_rows(state, query_groups, query_pos, key_block, value_block, key_pos)

    row_peak, row_total, weighted = lax.cond(
        jnp.int32(0) > last_query, skipped, worked, start_state
    )
    attended = (
        (weighted / row_total[..., None])
        .transpose(2, 0, 1, 3)
        .reshape(block_rows, query_width)
        .astype(jnp.bfloat16)
    )
    selected = attended
    projected = lax.psum_scatter(
        jnp.dot(selected, out_weight, preferred_element_type=jnp.float32).astype(jnp.bfloat16),
        "head",
        scatter_dimension=0,
        tiled=True,
    ).astype(jnp.float32)
    residual = (hidden_in.astype(jnp.float32) + projected).astype(jnp.bfloat16)
    widened = residual.astype(jnp.float32)
    mean_square = jnp.mean(widened * widened, axis=-1, keepdims=True)
    normed = (widened * lax.rsqrt(mean_square + 1e-05) * norm_gain).astype(jnp.bfloat16)
    shard_rows = lax.all_gather(normed, "head", axis=0, tiled=True)
    gate_part = jnp.dot(shard_rows, gate_weight, preferred_element_type=jnp.float32)
    up_part = jnp.dot(shard_rows, up_weight, preferred_element_type=jnp.float32)
    inner_act = (jax.nn.silu(gate_part) * up_part).astype(jnp.bfloat16)
    selected = inner_act
    mlp_out = lax.psum_scatter(
        jnp.dot(selected, down_weight, preferred_element_type=jnp.float32).astype(jnp.bfloat16),
        "head",
        scatter_dimension=0,
        tiled=True,
    ).astype(jnp.float32)
    return (residual.astype(jnp.float32) + mlp_out).astype(jnp.bfloat16)


def solution(mesh):
    return jax.shard_map(
        local,
        mesh=mesh,
        in_specs=(
            P(("blk", "head"), None),
            P(("blk", "head"), None),
            P(("blk", "head"), None),
            P(("blk", "head"), None),
            P("head", None),
            P(),
            P(None, "head"),
            P(None, "head"),
            P("head", None),
        ),
        out_specs=P(("blk", "head"), None),
        check_vma=False,
    )
```

profile of v0, /device:TPU:24, one launch (start us, length us, event | category | flops | bytes accessed | tf_op | source)
XLA Modules:
  0.0 335.4 jit_solution(1686048389370808473)
XLA Ops:
  6.5 1.7 copy_bitcast_fusion.2
  8.3 5.7 %all-to-all-start = ((bf16[64,8,128]{2,0,1:T(8,128)(2,1)}), bf16[64,8,128]{2,0,1:T(8,128)(2,1)S(1)}, u32[]{:S(2)}, u32[]{:S(2)}) async-start(bf16[64,8,128]{2,0,1:T(8,128)(2,1)} %copy_bitcast_fusion.2), calls=%async_computation | async-start | bytes 262144 | tf_op jit(solution)/shard_map/all_to_all | solution.py:60
  14.0 0.9 copy_bitcast_fusion.1
  14.9 5.6 %all-to-all-done = bf16[64,8,128]{2,0,1:T(8,128)(2,1)S(1)} async-done(((bf16[64,8,128]{2,0,1:T(8,128)(2,1)}), bf16[64,8,128]{2,0,1:T(8,128)(2,1)S(1)}, u32[]{:S(2)}, u32[]{:S(2)}) %all-to-all-start) | async-done | bytes 131104 | tf_op jit(solution)/shard_map/all_to_all | solution.py:60
  20.5 9.1 %all_to_all.54 = bf16[64,8,128]{2,0,1:T(8,128)(2,1)S(1)} all-to-all(bf16[64,8,128]{2,0,1:T(8,128)(2,1)S(1)} %copy_bitcast_fusion.1), channel_id=1, replica_groups=mesh['head'=8,'blk'=16] {'head'}, dimensions={1} | all-to-all | bytes 262144 | tf_op jit(solution)/shard_map/all_to_all | solution.py:61
  29.6 0.7 pad_maximum_fusion
  30.4 1.7 copy.39
  32.0 3.4 %all-to-all-start.2 = ((bf16[64,8,256]{2,0,1:T(8,128)(2,1)}), bf16[64,8,256]{2,0,1:T(8,128)(2,1)S(1)}, u32[]{:S(2)}, u32[]{:S(2)}) async-start(bf16[64,8,256]{2,0,1:T(8,128)(2,1)} %bitcast.70), calls=%async_computation.2 | async-start | bytes 524288 | tf_op jit(solution)/shard_map/all_to_all | solution.py:59
  35.5 7.2 %all-to-all-done.2 = bf16[64,8,256]{2,0,1:T(8,128)(2,1)S(1)} async-done(((bf16[64,8,256]{2,0,1:T(8,128)(2,1)}), bf16[64,8,256]{2,0,1:T(8,128)(2,1)S(1)}, u32[]{:S(2)}, u32[]{:S(2)}) %all-to-all-start.2) | async-done | bytes 262176 | tf_op jit(solution)/shard_map/all_to_all | solution.py:59
  42.7 43.6 %all-gather.3.cloned.1.call-done = bf16[8192,256]{1,0:T(8,128)(2,1)} async-done(((bf16[512,256]{1,0:T(8,128)(2,1)}), bf16[8192,256]{1,0:T(8,128)(2,1)}) %all-gather.3.cloned.1.call-update) | async-done | bytes 4194320 | tf_op jit(solution)/shard_map/all_gather | solution.py:20
  86.3 51.3 %conditional.1 = (f32[1,2,512]{2,1,0:T(2,128)S(1)}, f32[1,2,512,128]{2,3,1,0:T(8,128)S(1)}) conditional(s32[]{:T(128)} %convert_element_type.47, (s32[8192]{0:T(1024)S(1)}, s32[]{:T(128)}, s32[512]{0:T(512)S(1)}, bf16[8192,256]{1,0:T(8,128)(2,1)}, bf16[8,64,256]{2,1,0:T(8,128)(2,1)S(1)}) %tuple.29, () %tuple.14), branch_computations={%region_0.3_spmd, %region_3.4_spmd} | conditional | flops 4391435776 | bytes 139786288 | solution.py:86
  86.4 3.7 %broadcast_compare_fusion = pred[512,8192]{0,1:T(8,128)(4,1)S(1)} fusion(s32[512]{0:T(512)S(1)} %broadcast_add_fusion, s32[8192]{0:T(1024)S(1)} %get-tuple-element.21), kind=kLoop, calls=%fused_computation.10 | loop fusion | flops 4194304 | bytes 4229120 | tf_op jit(solution)/shard_map/cond/branch_0_fun/le | solution.py:33
  90.2 16.5 %fusion = (f32[2,512]{1,0:T(2,128)S(1)}, f32[8192,512,2]{1,0,2:T(8,128)}) fusion(pred[512,8192]{0,1:T(8,128)(4,1)S(1)} %broadcast_compare_fusion, bf16[512,2,128]{2,1,0:T(2,128)(2,1)S(1)} %reshape.53, bf16[8192,256]{1,0:T(8,128)(2,1)} %get-tuple-element.24), kind=kOutput, calls=%fused_computation.2 | convolution fusion | flops 2172648448 | bytes 40112128 | tf_op jit(solution)/shard_map/cond/branch_0_fun/qgrd,kgd->grqk/dot_general | solution.py:30
  106.7 15.9 %fusion.14 = f32[1,2,512,128]{2,3,1,0:T(8,128)S(1)} fusion(bf16[8192,256]{1,0:T(8,128)(2,1)} %get-tuple-element.24, f32[8192,512,2]{1,0,2:T(8,128)} %get-tuple-element.37, f32[2,512]{1,0:T(2,128)S(1)} %broadcast_maximum_fusion, pred[512,8192]{0,1:T(8,128)(4,1)} %copy-done.1), kind=kOutput, calls=%fused_computation.16 | convolution fusion | flops 2181038080 | bytes 40374272 | tf_op jit(solution)/shard_map/cond/branch_0_fun/grqk,kgd->grqd/dot_general | solution.py:37
  122.6 15.1 %fusion.4 = f32[2,512]{1,0:T(2,128)S(1)} fusion(f32[8192,512,2]{1,0,2:T(8,128)} %get-tuple-element.37, f32[2,512]{1,0:T(2,128)S(1)} %broadcast_maximum_fusion, pred[512,8192]{0,1:T(8,128)(4,1)} %copy-done.1), kind=kLoop, calls=%fused_computation.6 | loop fusion | flops 33553408 | bytes 37756928 | tf_op jit(solution)/shard_map/cond/branch_0_fun/reduce_sum | solution.py:36
  137.8 3.2 convolution_convert_fusion.1
  141.1 52.1 %reduce-scatter.3.cloned.1.call-done = bf16[64,4096]{1,0:T(8,128)(2,1)} async-done(((bf16[512,4096]{1,0:T(8,128)(2,1)}), bf16[64,4096]{1,0:T(8,128)(2,1)}) %reduce-scatter.3.cloned.1.call-update) | async-done | bytes 524304 | tf_op jit(solution)/shard_map/reduce_scatter | solution.py:96
  193.2 1.3 fusion.22
  194.6 2.0 fusion.24
  196.9 51.3 %all-gather.5.cloned.1.call-done = bf16[512,4096]{1,0:T(8,128)(2,1)} async-done(((bf16[64,4096]{1,0:T(8,128)(2,1)}), bf16[512,4096]{1,0:T(8,128)(2,1)}) %all-gather.5.cloned.1.call-update) | async-done | bytes 4194320 | tf_op jit(solution)/shard_map/all_gather | solution.py:106
  248.1 10.1 %fusion.27 = f32[512,896]{1,0:T(8,128)} fusion(bf16[512,4096]{1,0:T(8,128)(2,1)} %all-gather.5.cloned.1.call-done, bf16[4096,896]{1,0:T(8,128)(2,1)} %param.17), kind=kOutput, calls=%fused_computation.40 | convolution fusion | flops 3758096384 | bytes 13369344 | tf_op jit(solution)/shard_map/dot_general | solution.py:107
  258.2 16.6 %convolution_convert_fusion = bf16[512,4096]{1,0:T(8,128)(2,1)} fusion(bf16[896,4096]{1,0:T(8,128)(2,1)} %param.19, f32[512,896]{1,0:T(8,128)} %fusion.27, bf16[512,4096]{1,0:T(8,128)(2,1)} %all-gather.5.cloned.1.call-done, bf16[4096,896]{1,0:T(8,128)(2,1)} %param.18), kind=kOutput, calls=%fused_computation.22 | convolution fusion | flops 7521042432 | bytes 24903680 | tf_op jit(solution)/shard_map/dot_general | solution.py:112
  274.9 52.0 %reduce-scatter.5.cloned.1.call-done = bf16[64,4096]{1,0:T(8,128)(2,1)} async-done(((bf16[512,4096]{1,0:T(8,128)(2,1)}), bf16[64,4096]{1,0:T(8,128)(2,1)}) %reduce-scatter.5.cloned.1.call-update) | async-done | bytes 524304 | tf_op jit(solution)/shard_map/reduce_scatter | solution.py:111
  326.9 2.0 fusion.25
  (25 shorter events, 0.6 us)
Async XLA Ops:
  6.5 131.2 %copy-start = (bf16[256,4096]{1,0:T(8,128)(2,1)S(1)}, bf16[256,4096]{1,0:T(8,128)(2,1)}, u32[]{:S(2)}) copy-start(bf16[256,4096]{1,0:T(8,128)(2,1)} %param.15) | copy-start | bytes 6291460
  8.3 12.2 %all-to-all-start = ((bf16[64,8,128]{2,0,1:T(8,128)(2,1)}), bf16[64,8,128]{2,0,1:T(8,128)(2,1)S(1)}, u32[]{:S(2)}, u32[]{:S(2)}) async-start(bf16[64,8,128]{2,0,1:T(8,128)(2,1)} %copy_bitcast_fusion.2), calls=%async_computation | async-start | bytes 262144 | tf_op jit(solution)/shard_map/all_to_all | solution.py:60
  13.9 72.4 %all-gather.3.cloned.1.call-start = ((), (), s32[]{:S(2)}) async-start(), calls=%async_computation.5 | async-start | bytes 4456448 | tf_op jit(solution)/shard_map/all_gather | solution.py:20
  32.0 10.6 %all-to-all-start.2 = ((bf16[64,8,256]{2,0,1:T(8,128)(2,1)}), bf16[64,8,256]{2,0,1:T(8,128)(2,1)S(1)}, u32[]{:S(2)}, u32[]{:S(2)}) async-start(bf16[64,8,256]{2,0,1:T(8,128)(2,1)} %bitcast.70), calls=%async_computation.2 | async-start | bytes 524288 | tf_op jit(solution)/shard_map/all_to_all | solution.py:59
  35.5 157.7 %reduce-scatter.3.cloned.1.call-start = ((), (), s32[]{:S(2)}) async-start(), calls=%async_computation.6 | async-start | bytes 4718592 | tf_op jit(solution)/shard_map/reduce_scatter | solution.py:96
  90.1 16.5 %copy-start.1 = (pred[512,8192]{0,1:T(8,128)(4,1)}, pred[512,8192]{0,1:T(8,128)(4,1)S(1)}, u32[]{:S(2)}) copy-start(pred[512,8192]{0,1:T(8,128)(4,1)S(1)} %broadcast_compare_fusion) | copy-start | bytes 12582916 | tf_op jit(solution)/shard_map/cond
  137.7 55.6 %copy-start.2 = (bf16[64,4096]{1,0:T(8,128)(2,1)S(1)}, bf16[64,4096]{1,0:T(8,128)(2,1)}, u32[]{:S(2)}) copy-start(bf16[64,4096]{1,0:T(8,128)(2,1)} %param.11) | copy-start | bytes 1572868
  137.7 56.9 %copy-start.4 = (f32[4096]{0:T(1024)S(1)}, f32[4096]{0:T(1024)}, u32[]{:S(2)}) copy-start(f32[4096]{0:T(1024)} %param.16) | copy-start | bytes 49156
  141.0 107.1 %all-gather.5.cloned.1.call-start = ((), (), s32[]{:S(2)}) async-start(), calls=%async_computation.7 | async-start | bytes 4718592 | tf_op jit(solution)/shard_map/all_gather | solution.py:106
  196.6 130.3 %reduce-scatter.5.cloned.1.call-start = ((), (), s32[]{:S(2)}) async-start(), calls=%async_computation.8 | async-start | bytes 4718592 | tf_op jit(solution)/shard_map/reduce_scatter | solution.py:111
  258.2 68.6 %copy-start.3 = (bf16[64,4096]{1,0:T(8,128)(2,1)S(1)}, bf16[64,4096]{1,0:T(8,128)(2,1)}, u32[]{:S(2)}) copy-start(bf16[64,4096]{1,0:T(8,128)(2,1)} %reduce-scatter.3.cloned.1.call-done) | copy-start | bytes 1572868
Sparse Core Ops, SparseCore 0:
  30.5 55.7 all-gather.2
  141.1 52.0 reduce-scatter.2
  196.7 51.3 all-gather.4
  275.0 51.8 reduce-scatter.4
where the time goes:
time: 337 us; the launch traced here: 335 us
  waiting for transfers between devices  212 us (63%)
  matrix products  62.3 us (18%)
  other arithmetic  25 us (7%)
  between operations  13.2 us (4%)
  starting transfers between devices  9.41 us (3%)
  blocking collectives  9.1 us (3%)
  local copies, waits for them, and re-layouts  4.43 us (1%)
    reduce_scatter x1, waiting for transfers between devices, local(): lax.psum_scatter(jnp.dot(selected, out_weight, preferred_element_type=jnp...  52.1 us
    reduce_scatter x1, waiting for transfers between devices, local(): lax.psum_scatter(jnp.dot(selected, down_weight, preferred_element_type=jn...  52 us
    all_gather x1, waiting for transfers between devices, local(): shard_rows = lax.all_gather(normed, 'head', axis=0, tiled=True)  51.3 us
    all_gather x1, waiting for transfers between devices, sent_together(): lax.all_gather(both, axis, axis=dim, tiled=True)  43.6 us
    dot_general x1, matrix products, local(): jnp.dot(selected, down_weight, preferred_element_type=jnp.float32)  16.6 us
    dot_general x1, matrix products, absorb_rows(): jnp.einsum('qgrd,kgd->grqk', query_groups, key_heads, preferred_element_t...  16.5 us
    dot_general x1, matrix products, absorb_rows(): jnp.einsum('grqk,kgd->grqd', exp_scores.astype(jnp.bfloat16), value_heads...  15.9 us
    reduce_sum x1, other arithmetic, absorb_rows(): new_total = jnp.sum(exp_scores, axis=-1)  15.1 us
  transfers between devices with their start and end apart: 6, of which 6 were waited for; matrix products, arithmetic and copies ran while one was open for 1% of the time, Pallas kernels for 0%

commit v1 on v0

v1 whole, which is shorter than its diff:
```python
import jax
import jax.numpy as jnp
from jax import lax
from jax.experimental import pallas as pl
from jax.experimental.pallas import tpu as pltpu
from jax.sharding import PartitionSpec as P

HEADS = 16
KV_HEADS = 8
HEAD_DIM = 128
MESH = pl.DeviceIdType.MESH
F32 = jnp.float32
BF16 = jnp.bfloat16

negative_fill = -1e30


class Place:
    def __init__(self):
        self.head = lax.axis_index("head")
        self.blk = lax.axis_index("blk")
        self.x = lax.rem(self.head, 4)
        self.zl = self.head // 4
        self.zh = self.blk // 8
        self.yc = lax.rem(self.blk, 8)
        self.z = self.zh * 2 + self.zl
        self.xs = [lax.rem(self.x + k, 4) for k in range(4)]
        self.right = self.at_x(self.xs[1])
        self.left = self.at_x(self.xs[3])
        self.above = self.at_z(1)
        self.below = self.at_z(3)

    def at_x(self, x):
        return (self.zl * 4 + x, self.blk)

    def at_z(self, step):
        z = lax.rem(self.z + step, 4)
        return (lax.rem(z, 2) * 4 + self.x, (z // 2) * 8 + self.yc)

    def here(self, k):
        return self.zl * 4 + self.xs[k]

    def other(self, k):
        return (1 - self.zl) * 4 + self.xs[k]


def remote(src, dst, send_sem, recv_sem, device):
    return pltpu.make_async_remote_copy(
        src_ref=src, dst_ref=dst, send_sem=send_sem, recv_sem=recv_sem,
        device_id=device, device_id_type=MESH,
    )


def gather_rows(p, buf, send_sem, recv, steps, compute):
    def send(h, s, half, to_half, kind, device):
        remote(buf.at[h, s, half], buf.at[h, s, to_half], send_sem, recv.at[kind, s], device).start()

    def wait(h, s, half, kind):
        remote(buf.at[h, s, half], buf.at[h, s, half], send_sem, recv.at[kind, s], p.right).wait_recv()

    me, left, right, far = p.here(0), p.here(3), p.here(1), p.here(2)
    for s in range(steps):
        send(me, s, 0, 0, 0, p.right)
        send(me, s, 1, 1, 4, p.left)
        send(me, s, 0, 1, 6, p.above)
        send(me, s, 1, 0, 10, p.below)
    for s in range(steps):
        send(me, s, 1, 1, 1, p.right)
        send(me, s, 0, 0, 3, p.left)
    compute(me, True)
    for s in range(steps):
        wait(left, s, 0, 0)
        send(left, s, 0, 0, 2, p.right)
        send(left, s, 0, 1, 7, p.above)
        wait(right, s, 1, 4)
        send(right, s, 1, 1, 5, p.left)
        send(right, s, 1, 0, 12, p.below)
    for s in range(steps):
        wait(p.other(0), s, 1, 6)
        wait(p.other(0), s, 0, 10)
    compute(p.other(0), False)
    for s in range(steps):
        wait(left, s, 1, 1)
        send(left, s, 1, 0, 11, p.below)
        wait(right, s, 0, 3)
        send(right, s, 0, 1, 8, p.above)
    compute(left, False)
    compute(right, False)
    for s in range(steps):
        wait(far, s, 0, 2)
        send(far, s, 0, 1, 9, p.above)
        wait(far, s, 1, 5)
        send(far, s, 1, 0, 13, p.below)
    compute(far, False)
    for k, up, down in ((3, 7, 11), (1, 8, 12), (2, 9, 13)):
        for s in range(steps):
            wait(p.other(k), s, 1, up)
            wait(p.other(k), s, 0, down)
        compute(p.other(k), False)
    pltpu.make_async_copy(buf.at[0:7], buf.at[0:7], send_sem).wait()


NS1 = 2
NS2 = 4
NC = 8
CW = 512
FFL = 896


def block_kernel(
    att, hid, gain, wo_hbm, gate_hbm, up_hbm, down_hbm, out,
    abuf, rbuf, wo, wgu, wd, oacc, acc, xg, sq, inner,
    zs, zr, keep, m1s, m1r, m2s, m2r,
    wsem, s1, r1, s2, r2, s3, zsem, m1sem, m2sem,
):
    p = Place()
    barrier = pltpu.get_barrier_semaphore()
    for device in (p.right, p.left, p.above, p.below):
        pl.semaphore_signal(barrier, inc=1, device_id=device, device_id_type=MESH)

    order = [p.here(0), p.other(0), p.here(3), p.here(1), p.here(2), p.other(3), p.other(1), p.other(2)]
    wo_copy = pltpu.make_async_copy(wo_hbm, wo, wsem.at[16])
    wd_copy = pltpu.make_async_copy(down_hbm, wd, wsem.at[17])

    def gate_copy(h):
        rows = pl.ds(pl.multiple_of(h * 512, 512), 512)
        return pltpu.make_async_copy(gate_hbm.at[rows], wgu.at[rows, 0:FFL], wsem.at[h])

    def up_copy(h):
        rows = pl.ds(pl.multiple_of(h * 512, 512), 512)
        return pltpu.make_async_copy(up_hbm.at[rows], wgu.at[rows, FFL : 2 * FFL], wsem.at[8 + h])

    wo_copy.start()
    for h in order:
        gate_copy(h).start()
        up_copy(h).start()
    wd_copy.start()

    me = p.here(0)
    c1 = 256 // NS1
    for s in range(NS1):
        for half in range(2):
            abuf[me, s, half] = att[half * 256 : (half + 1) * 256, s * c1 : (s + 1) * c1]
    pl.semaphore_wait(barrier, 4)

    def project(h, first):
        if first:
            wo_copy.wait()
        a = jnp.concatenate([abuf[h, s].reshape(512, c1) for s in range(NS1)], axis=1)
        rows = pl.ds(pl.multiple_of(h * 256, 256), 256)
        for n in range(2):
            cols = slice(n * 256, (n + 1) * 256)
            part = jnp.dot(a, wo[rows, cols], preferred_element_type=F32)
            if first:
                oacc[:, cols] = hid[:, cols].astype(F32) + part
            else:
                oacc[:, cols] += part

    gather_rows(p, abuf, s1, r1, NS1, project)

    c2 = 512 // NS2
    for s in range(NS2):
        for half in range(2):
            rbuf[me, s, half] = oacc[half * 256 : (half + 1) * 256, s * c2 : (s + 1) * c2].astype(BF16)

    def expand(h, first):
        gate_copy(h).wait()
        up_copy(h).wait()
        total = None
        for s in range(NS2):
            r = rbuf[h, s].reshape(512, c2).astype(F32)
            g = gain[pl.ds(h * NS2 + s, 1), :]
            xg[:, s * c2 : (s + 1) * c2] = (r * g).astype(BF16)
            total = r * r if total is None else total + r * r
        if first:
            sq[...] = total
        else:
            sq[...] += total
        rows = pl.ds(pl.multiple_of(h * 512, 512), 512)

        def tile(n, _):
            cols = pl.ds(pl.multiple_of(n * 256, 256), 256)
            part = jnp.dot(xg[...], wgu[rows, cols], preferred_element_type=F32)
            if first:
                acc[:, cols] = part
            else:
                acc[:, cols] += part
            return 0

        lax.fori_loop(0, 7, tile, 0)

    gather_rows(p, rbuf, s2, r2, NS2, expand)

    scale = lax.rsqrt(jnp.sum(sq[...], axis=1, keepdims=True) * (1.0 / 4096.0) + 1e-5)
    sq[...] = jnp.broadcast_to(scale, (512, 128))

    def activate(j, _):
        at = pl.multiple_of(j * 128, 128)
        u = acc[:, pl.ds(at, 128)] * sq[...]
        v = acc[:, pl.ds(pl.multiple_of(at + FFL, 128), 128)] * sq[...]
        inner[:, pl.ds(at, 128)] = (u / (1.0 + jnp.exp(-u)) * v).astype(BF16)
        return 0

    lax.fori_loop(0, 7, activate, 0)

    def z_copy(c, side):
        device = p.above if side == 0 else p.below
        return remote(zs.at[c, side], zr.at[c, 1 - side], s3, zsem.at[1 - side, c], device)

    def z_wait(c, side):
        remote(zr.at[c, side], zr.at[c, side], s3, zsem.at[side, c], p.right).wait_recv()

    def reduce_down(c, _):
        for n in range(2):
            at = slice(n * 256, (n + 1) * 256)
            cols = pl.ds(pl.multiple_of(c * CW + n * 256, 256), 256)
            part = jnp.dot(inner[...], wd[:, cols], preferred_element_type=F32)
            keep[c, 0, :, at] = part[0:128]
            zs[c, 0, :, at] = part[128:256].astype(BF16)
            zs[c, 1, :, at] = part[256:384].astype(BF16)
            keep[c, 1, :, at] = part[384:512]
        z_copy(c, 0).start()
        z_copy(c, 1).start()
        return 0

    wd_copy.wait()
    lax.fori_loop(0, NC, reduce_down, 0)

    def slot(k):
        return pl.ds(pl.multiple_of(p.xs[k] * 32, 32), 32)

    def m1_copy(c, side):
        device = p.right if side == 0 else p.left
        return remote(m1s.at[c, side], m1r.at[c, side], s3, m1sem.at[side, c], device)

    def m2_copy(c, side):
        device = p.right if side == 0 else p.left
        return remote(m2s.at[c, side], m2r.at[c, side], s3, m2sem.at[side, c], device)

    def finish(t, _):
        @pl.when(t < NC)
        def _():
            c = t
            for side in range(2):
                z_wait(c, side)
                keep[c, side] += zr[c, side].astype(F32)
                m1s[c, side] = keep[c, side, slot(2), :].astype(BF16)
                m1_copy(c, side).start()

        @pl.when((t >= 1) & (t < NC + 1))
        def _():
            c = t - 1
            for side in range(2):
                m1_copy(c, side).wait_recv()
                k = 1 if side == 0 else 3
                for part in range(2):
                    q = keep[c, part, slot(k), :]
                    if part == side:
                        q = q + m1r[c, side].astype(F32)
                    m2s[c, side, part] = q.astype(BF16)
                m2_copy(c, side).start()

        @pl.when(t >= 2)
        def _():
            c = t - 2
            for side in range(2):
                m2_copy(c, side).wait_recv()
            for part in range(2):
                q = keep[c, part, slot(0), :] + m2r[c, 0, part].astype(F32) + m2r[c, 1, part].astype(F32)
                rows = pl.ds(pl.multiple_of(part * 128 + p.x * 32, 32), 32)
                for s in range(NS2):
                    r = rbuf[c, s, part, rows, :].astype(F32)
                    cols = pl.ds(pl.multiple_of(c * CW + s * c2, c2), c2)
                    out[part * 32 : (part + 1) * 32, cols] = (r + q[:, s * c2 : (s + 1) * c2]).astype(BF16)

        return 0

    lax.fori_loop(0, NC + 2, finish, 0)
    pltpu.make_async_copy(zs, zs, s3).wait()
    pltpu.make_async_copy(m1s, m1s, s3).wait()
    pltpu.make_async_copy(m2s, m2s, s3).wait()


def feed_forward(att, hid, wo, gain, gate, up, down):
    vmem = pl.BlockSpec(memory_space=pltpu.VMEM)
    hbm = pl.BlockSpec(memory_space=pl.ANY)
    dma = pltpu.SemaphoreType.DMA
    return pl.pallas_call(
        block_kernel,
        out_shape=jax.ShapeDtypeStruct((64, 4096), BF16),
        in_specs=[vmem, vmem, vmem, hbm, hbm, hbm, hbm],
        out_specs=vmem,
        scratch_shapes=[
            pltpu.VMEM((8, NS1, 2, 256, 256 // NS1), BF16),
            pltpu.VMEM((8, NS2, 2, 256, 512 // NS2), BF16),
            pltpu.VMEM((2048, 512), BF16),
            pltpu.VMEM((4096, 2 * FFL), BF16),
            pltpu.VMEM((FFL, 4096), BF16),
            pltpu.VMEM((512, 512), F32),
            pltpu.VMEM((512, 2 * FFL), F32),
            pltpu.VMEM((512, 512), BF16),
            pltpu.VMEM((512, 128), F32),
            pltpu.VMEM((512, FFL), BF16),
            pltpu.VMEM((NC, 2, 128, CW), BF16),
            pltpu.VMEM((NC, 2, 128, CW), BF16),
            pltpu.VMEM((NC, 2, 128, CW), F32),
            pltpu.VMEM((NC, 2, 32, CW), BF16),
            pltpu.VMEM((NC, 2, 32, CW), BF16),
            pltpu.VMEM((NC, 2, 2, 32, CW), BF16),
            pltpu.VMEM((NC, 2, 2, 32, CW), BF16),
            dma((18,)),
            dma,
            dma((14, NS1)),
            dma,
            dma((14, NS2)),
            dma,
            dma((2, NC)),
            dma((2, NC)),
            dma((2, NC)),
        ],
        compiler_params=pltpu.CompilerParams(
            collective_id=1, has_side_effects=True, vmem_limit_bytes=62 * 1024 * 1024
        ),
        cost_estimate=pl.CostEstimate(flops=12_500_000_000, bytes_accessed=24_000_000, transcendentals=0),
        name="feed_forward",
    )(att, hid, gain, wo, gate, up, down)


def sent_together(arrays, axis, dim, along):
    ends, at = ([], 0)
    for a in arrays[:-1]:
        at += a.shape[along]
        ends.append(at)
    both = jnp.concatenate(arrays, axis=along)
    return tuple(jnp.split(lax.all_gather(both, axis, axis=dim, tiled=True), ends, axis=along))


def absorb_rows(query_groups, query_pos, key_block, value_block, key_pos):
    key_count = key_block.shape[0]
    group_count = query_groups.shape[1]
    head_size = query_groups.shape[3]
    key_heads = key_block.reshape(key_count, group_count, head_size)
    value_heads = value_block.reshape(key_count, group_count, head_size)
    scores = jnp.einsum(
        "qgrd,kgd->grqk", query_groups, key_heads, preferred_element_type=jnp.float32
    ) * head_size ** (-0.5)
    visible = key_pos[None, :] <= query_pos[:, None]
    new_peak = jnp.max(jnp.where(visible, scores, negative_fill), axis=-1)
    exp_scores = jnp.where(visible, jnp.exp(scores - new_peak[..., None]), 0.0)
    new_total = jnp.sum(exp_scores, axis=-1)
    products = jnp.einsum(
        "grqk,kgd->grqd",
        exp_scores.astype(jnp.bfloat16),
        value_heads,
        preferred_element_type=jnp.float32,
    )
    return new_total, products


def regroup(rows):
    width = rows.shape[1]
    zl = lax.axis_index("head") // 4
    parts = rows.reshape(2, 4, 2, 32, width)
    own = jnp.where(zl == 0, parts[0], parts[1])
    other = jnp.where(zl == 0, parts[1], parts[0])
    gives = jnp.where(zl == 0, other[:, 0], other[:, 1]).reshape(128, width)
    keeps = jnp.where(zl == 0, other[:, 1], other[:, 0]).reshape(128, width)
    gets = lax.ppermute(gives, "blk", [(b, (b + 8) % 16) for b in range(16)])
    upper = jnp.where(zl == 0, keeps, gets)
    lower = jnp.where(zl == 0, gets, keeps)
    return jnp.concatenate([own[:, 0].reshape(128, width), upper, lower, own[:, 1].reshape(128, width)], axis=0)


def local(
    hidden_in,
    queries,
    key_states,
    value_states,
    out_weight,
    norm_gain,
    gate_weight,
    up_weight,
    down_weight,
):
    own_block = lax.axis_index("blk")
    query_local, key_local, value_local = (
        lax.all_to_all(queries, "head", split_axis=1, concat_axis=0, tiled=True),
        lax.all_to_all(key_states, "head", split_axis=1, concat_axis=0, tiled=True),
        lax.all_to_all(value_states, "head", split_axis=1, concat_axis=0, tiled=True),
    )
    hidden_local = lax.all_to_all(hidden_in, "head", split_axis=1, concat_axis=0, tiled=True)
    wo = lax.all_to_all(out_weight, "head", split_axis=1, concat_axis=0, tiled=True)
    block_rows = query_local.shape[0]
    query_width = query_local.shape[1]
    key_width = key_local.shape[1]
    group_count = key_width // HEAD_DIM
    group_ratio = HEADS // KV_HEADS
    local_index = jnp.arange(block_rows, dtype=jnp.int32)
    query_pos = own_block * block_rows + local_index
    query_groups = query_local.reshape(block_rows, group_count, group_ratio, HEAD_DIM)
    key_block, value_block = sent_together((key_local, value_local), "blk", 0, 1)
    key_pos = jnp.arange(key_block.shape[0], dtype=jnp.int32)
    row_total, weighted = absorb_rows(query_groups, query_pos, key_block, value_block, key_pos)
    attended = (
        (weighted / row_total[..., None])
        .transpose(2, 0, 1, 3)
        .reshape(block_rows, query_width)
        .astype(jnp.bfloat16)
    )
    att = regroup(attended)
    hid = regroup(hidden_local)
    return feed_forward(att, hid, wo, norm_gain.reshape(4 * 8, 128), gate_weight, up_weight, down_weight)


def solution(mesh):
    return jax.shard_map(
        local,
        mesh=mesh,
        in_specs=(
            P(("blk", "head"), None),
            P(("blk", "head"), None),
            P(("blk", "head"), None),
            P(("blk", "head"), None),
            P("head", None),
            P(),
            P(None, "head"),
            P(None, "head"),
            P("head", None),
        ),
        out_specs=P(("blk", "head"), None),
        check_vma=False,
    )
```

time: 337 us -> 254 us (0.75)
  waiting for transfers between devices: 212 us -> 57.2 us
  Pallas kernels: 0 us -> 81 us
  matrix products: 62.3 us -> 33.7 us
  starting transfers between devices: 9.41 us -> 23 us
  local copies, waits for them, and re-layouts: 4.43 us -> 11.6 us
    reduce_scatter x2 -> x0, waiting for transfers between devices: 104 us -> none  [the longest x1 52.1 us: local(): lax.psum_scatter(jnp.dot(selected, out_weight, preferred_element_type=jnp...]
    pallas_call x0 -> x1, Pallas kernels: none -> 81 us  [feed_forward(): pl.pallas_call(block_kernel, out_shape=jax.ShapeDtypeStruct((64, 4096), B...]
    all_gather x1 -> x0, waiting for transfers between devices: 51.3 us -> none  [local(): shard_rows = lax.all_gather(normed, 'head', axis=0, tiled=True)]
    ppermute x0 -> x2, waiting for transfers between devices: none -> 34.8 us  [regroup(): gets = lax.ppermute(gives, 'blk', [(b, (b + 8) % 16) for b in range(16)])]
    all_gather x1, waiting for transfers between devices: 43.6 us -> 11.4 us  [sent_together(): lax.all_gather(both, axis, axis=dim, tiled=True)]
    dot_general x3 -> x0, matrix products: 29.9 us -> none  [the longest x1 16.6 us: local(): jnp.dot(selected, down_weight, preferred_element_type=jnp.float32)]
    all_to_all x0 -> x2, starting transfers between devices: none -> 9.14 us  [the longest x1 5.64 us: local(): lax.all_to_all(out_weight, 'head', split_axis=1, concat_axis=0, tiled=True)]
    all_to_all x0 -> x2, local copies, waits for them, and re-layouts: none -> 4.98 us  [the longest x1 3.09 us: local(): lax.all_to_all(out_weight, 'head', split_axis=1, concat_axis=0, tiled=True)]
  transfers between devices with their start and end apart: 6 -> 7, of which waited for: 6 -> 5; matrix products, arithmetic and copies ran while one was open for 1% -> 25% of each run, Pallas kernels for 0% -> 0%
where the time goes in v1:
time: 254 us; the launch traced here: 252 us
  Pallas kernels  81 us (32%)
  waiting for transfers between devices  57.2 us (23%)
  matrix products  33.7 us (13%)
  starting transfers between devices  23 us (9%)
  other arithmetic  22.8 us (9%)
  between operations  13.5 us (5%)
  local copies, waits for them, and re-layouts  11.6 us (5%)
  blocking collectives  9.1 us (4%)
    pallas_call x1, Pallas kernels, feed_forward(): pl.pallas_call(block_kernel, out_shape=jax.ShapeDtypeStruct((64, 4096), B...  81 us
    ppermute x2, waiting for transfers between devices, regroup(): gets = lax.ppermute(gives, 'blk', [(b, (b + 8) % 16) for b in range(16)])  34.8 us
    dot_general x1, matrix products, absorb_rows(): jnp.einsum('grqk,kgd->grqd', exp_scores.astype(jnp.bfloat16), value_heads...  18 us
    dot_general x1, matrix products, absorb_rows(): jnp.einsum('qgrd,kgd->grqk', query_groups, key_heads, preferred_element_t...  15.7 us
    reduce_sum x1, other arithmetic, absorb_rows(): new_total = jnp.sum(exp_scores, axis=-1)  14.9 us
    all_gather x1, waiting for transfers between devices, sent_together(): lax.all_gather(both, axis, axis=dim, tiled=True)  11.4 us
    all_to_all x1, blocking collectives, local(): lax.all_to_all(value_states, 'head', split_axis=1, concat_axis=0, tiled=T...  9.1 us
    all_to_all x1, starting transfers between devices, local(): lax.all_to_all(key_states, 'head', split_axis=1, concat_axis=0, tiled=True)  5.65 us
  transfers between devices with their start and end apart: 7, of which 5 were waited for; matrix products, arithmetic and copies ran while one was open for 25% of the time, Pallas kernels for 0%

profile of v1, /device:TPU:24, one launch (start us, length us, event | category | flops | bytes accessed | tf_op | source)
XLA Modules:
  0.0 251.8 jit_solution(12768717401460730053)
XLA Ops:
  6.5 0.9 copy-done
  8.1 5.7 %all-to-all-start = ((bf16[64,8,128]{2,0,1:T(8,128)(2,1)}), bf16[64,8,128]{2,0,1:T(8,128)(2,1)S(1)}, u32[]{:S(2)}, u32[]{:S(2)}) async-start(bf16[64,8,128]{2,0,1:T(8,128)(2,1)} %copy_bitcast_fusion.4), calls=%async_computation | async-start | bytes 262144 | tf_op jit(solution)/shard_map/all_to_all | solution.py:388
  13.8 0.9 copy_bitcast_fusion.3
  14.8 5.6 %all-to-all-done = bf16[64,8,128]{2,0,1:T(8,128)(2,1)S(1)} async-done(((bf16[64,8,128]{2,0,1:T(8,128)(2,1)}), bf16[64,8,128]{2,0,1:T(8,128)(2,1)S(1)}, u32[]{:S(2)}, u32[]{:S(2)}) %all-to-all-start) | async-done | bytes 131104 | tf_op jit(solution)/shard_map/all_to_all | solution.py:388
  20.4 9.1 %all_to_all.89 = bf16[64,8,128]{2,0,1:T(8,128)(2,1)S(1)} all-to-all(bf16[64,8,128]{2,0,1:T(8,128)(2,1)S(1)} %copy_bitcast_fusion.3), channel_id=1, replica_groups=mesh['head'=8,'blk'=16] {'head'}, dimensions={1} | all-to-all | bytes 262144 | tf_op jit(solution)/shard_map/all_to_all | solution.py:389
  30.2 1.7 copy.58
  31.9 3.4 %all-to-all-start.2 = ((bf16[64,8,256]{2,0,1:T(8,128)(2,1)}), bf16[64,8,256]{2,0,1:T(8,128)(2,1)S(1)}, u32[]{:S(2)}, u32[]{:S(2)}) async-start(bf16[64,8,256]{2,0,1:T(8,128)(2,1)} %bitcast.102), calls=%async_computation.2 | async-start | bytes 524288 | tf_op jit(solution)/shard_map/all_to_all | solution.py:387
  35.3 1.9 copy.57
  37.2 5.3 %all-to-all-done.2 = bf16[64,8,256]{2,0,1:T(8,128)(2,1)S(1)} async-done(((bf16[64,8,256]{2,0,1:T(8,128)(2,1)}), bf16[64,8,256]{2,0,1:T(8,128)(2,1)S(1)}, u32[]{:S(2)}, u32[]{:S(2)}) %all-to-all-start.2) | async-done | bytes 262176 | tf_op jit(solution)/shard_map/all_to_all | solution.py:387
  42.5 3.5 %all-to-all-start.3 = ((bf16[64,8,512]{2,0,1:T(8,128)(2,1)}), bf16[64,8,512]{2,0,1:T(8,128)(2,1)S(1)}, u32[]{:S(2)}, u32[]{:S(2)}) async-start(bf16[64,8,512]{2,0,1:T(8,128)(2,1)} %bitcast.101), calls=%async_computation.3 | async-start | bytes 1048576 | tf_op jit(solution)/shard_map/all_to_all | solution.py:391
  46.0 5.5 %iota_compare_fusion = pred[512,8192]{0,1:T(8,128)(4,1)} fusion(s32[512]{0:T(512)S(1)} %iota_add_fusion), kind=kLoop, calls=%fused_computation.8 | loop fusion | flops 4194304 | bytes 4196352 | tf_op jit(solution)/shard_map/le | solution.py:347
  51.5 3.1 %copy.56 = bf16[32,8,8,512]{3,2,0,1:T(8,128)(2,1)} copy(bf16[32,8,8,512]{3,2,1,0:T(8,128)(2,1)} %bitcast.103) | data formatting | bytes 4194304 | tf_op jit(solution)/shard_map/all_to_all | solution.py:392
  54.7 5.6 %all-to-all-start.4 = ((bf16[256,8,512]{2,0,1:T(8,128)(2,1)}), bf16[256,8,512]{2,0,1:T(8,128)(2,1)}, u32[]{:S(2)}, u32[]{:S(2)}) async-start(bf16[256,8,512]{2,0,1:T(8,128)(2,1)} %bitcast.100), calls=%async_computation.4 | async-start | bytes 4194304 | tf_op jit(solution)/shard_map/all_to_all | solution.py:392
  60.4 3.9 %collective-permute-start.1 = (bf16[128,512]{1,0:T(8,128)(2,1)S(1)}, bf16[128,512]{1,0:T(8,128)(2,1)S(1)}, u32[]{:S(2)}, u32[]{:S(2)}) collective-permute-start(bf16[128,512]{1,0:T(8,128)(2,1)S(1)} %bitcast.116), channel_id=1, source_target_pairs={{0,8},{1,9},{2,10},{3,11},{4,12},{5,13},{6,14},{7,15},{8,0},{9,1},... | collective-permute-start | bytes 393224 | tf_op jit(solution)/shard_map/ppermute | solution.py:368
  64.3 29.9 %collective-permute-done.1 = bf16[128,512]{1,0:T(8,128)(2,1)S(1)} collective-permute-done((bf16[128,512]{1,0:T(8,128)(2,1)S(1)}, bf16[128,512]{1,0:T(8,128)(2,1)S(1)}, u32[]{:S(2)}, u32[]{:S(2)}) %collective-permute-start.1) | collective-permute-done | bytes 131104 | tf_op jit(solution)/shard_map/ppermute | solution.py:368
  94.2 0.8 pad_maximum_fusion.hid
  95.0 11.4 %all-gather.2.cloned.1.call-done = bf16[8192,256]{1,0:T(8,128)(2,1)} async-done(((bf16[512,256]{1,0:T(8,128)(2,1)}), bf16[8192,256]{1,0:T(8,128)(2,1)}) %all-gather.2.cloned.1.call-update) | async-done | bytes 4194320 | tf_op jit(solution)/shard_map/all_gather | solution.py:335
  106.4 15.7 %fusion = (f32[2,512]{1,0:T(2,128)S(1)}, f32[8192,512,2]{1,0,2:T(8,128)}) fusion(pred[512,8192]{0,1:T(8,128)(4,1)} %iota_compare_fusion, bf16[512,2,128]{2,1,0:T(2,128)(2,1)S(1)} %reshape.102, bf16[8192,256]{1,0:T(8,128)(2,1)} %all-gather.2.cloned.1.call-done), kind=kOutput, calls=%fused_computation.2 | convolution fusion | flops 2172648448 | bytes 40112128 | tf_op jit(solution)/shard_map/qgrd,kgd->grqk/dot_general | solution.py:344
  122.1 14.9 %fusion.3 = f32[2,512]{1,0:T(2,128)S(1)} fusion(f32[8192,512,2]{1,0,2:T(8,128)} %get-tuple-element.22, f32[2,512]{1,0:T(2,128)S(1)} %get-tuple-element.21, pred[512,8192]{0,1:T(8,128)(4,1)S(1)} %copy-done.2), kind=kLoop, calls=%fused_computation.5 | loop fusion | flops 33553408 | bytes 37756928 | tf_op jit(solution)/shard_map/reduce_sum | solution.py:350
  137.0 18.0 %fusion.16 = bf16[512,1,2,128]{3,0,2,1:T(8,128)(2,1)S(1)} fusion(bf16[8192,256]{1,0:T(8,128)(2,1)} %all-gather.2.cloned.1.call-done, f32[8192,512,2]{1,0,2:T(8,128)} %get-tuple-element.22, f32[2,512]{1,0:T(2,128)S(1)} %get-tuple-element.21, pred[512,8192]{0,1:T(8,128)(4,1)} %iota_compare_fusion, f32[2,512]{1,0:T(2,128)S(1)} %fusion.3), kind=kOutput, calls=%fused_computation.17 | convolution fusion | flops 2181300224 | bytes 40116224 | tf_op jit(solution)/shard_map/grqk,kgd->grqd/dot_general | solution.py:351
  155.3 0.9 collective-permute-start
  156.5 4.9 %collective-permute-done = bf16[128,256]{1,0:T(8,128)(2,1)S(1)} collective-permute-done((bf16[128,256]{1,0:T(8,128)(2,1)S(1)}, bf16[128,256]{1,0:T(8,128)(2,1)S(1)}, u32[]{:S(2)}, u32[]{:S(2)}) %collective-permute-start) | collective-permute-done | bytes 65568 | tf_op jit(solution)/shard_map/ppermute | solution.py:368
  162.2 81.0 %feed_forward.1 = bf16[64,4096]{1,0:T(8,128)(2,1)} custom-call(bf16[512,256]{1,0:T(8,128)(2,1)} %pad_maximum_fusion.2.att, bf16[512,512]{1,0:T(8,128)(2,1)} %pad_maximum_fusion.hid, f32[32,128]{1,0:T(8,128)} %bitcast.118, bf16[2048,512]{1,0:T(8,128)(2,1)} %bitcast.27.wo_hbm, bf16[4096,896]{1,0:T(8,128)(2,1)} %gate_hbm.1, bf16[4096,896]{1,0:T(8,128)(2,1)} %up_hbm.1, ...), custom_call_target="tpu_custom_call" | custom-call | flops 12499999744 | bytes 24000000 | tf_op jit(solution)/shard_map/feed_forward/pallas_call | solution.py:288
  243.1 1.9 copy.60
  (26 shorter events, 2.9 us)
Async XLA Ops:
  6.5 0.9 copy-start
  8.1 12.2 %all-to-all-start = ((bf16[64,8,128]{2,0,1:T(8,128)(2,1)}), bf16[64,8,128]{2,0,1:T(8,128)(2,1)S(1)}, u32[]{:S(2)}, u32[]{:S(2)}) async-start(bf16[64,8,128]{2,0,1:T(8,128)(2,1)} %copy_bitcast_fusion.4), calls=%async_computation | async-start | bytes 262144 | tf_op jit(solution)/shard_map/all_to_all | solution.py:388
  13.8 92.6 %all-gather.2.cloned.1.call-start = ((), (), s32[]{:S(2)}) async-start(), calls=%async_computation.5 | async-start | bytes 4456448 | tf_op jit(solution)/shard_map/all_gather | solution.py:335
  31.9 10.6 %all-to-all-start.2 = ((bf16[64,8,256]{2,0,1:T(8,128)(2,1)}), bf16[64,8,256]{2,0,1:T(8,128)(2,1)S(1)}, u32[]{:S(2)}, u32[]{:S(2)}) async-start(bf16[64,8,256]{2,0,1:T(8,128)(2,1)} %bitcast.102), calls=%async_computation.2 | async-start | bytes 524288 | tf_op jit(solution)/shard_map/all_to_all | solution.py:387
  42.5 12.1 %all-to-all-start.3 = ((bf16[64,8,512]{2,0,1:T(8,128)(2,1)}), bf16[64,8,512]{2,0,1:T(8,128)(2,1)S(1)}, u32[]{:S(2)}, u32[]{:S(2)}) async-start(bf16[64,8,512]{2,0,1:T(8,128)(2,1)} %bitcast.101), calls=%async_computation.3 | async-start | bytes 1048576 | tf_op jit(solution)/shard_map/all_to_all | solution.py:391
  54.7 107.5 %all-to-all-start.4 = ((bf16[256,8,512]{2,0,1:T(8,128)(2,1)}), bf16[256,8,512]{2,0,1:T(8,128)(2,1)}, u32[]{:S(2)}, u32[]{:S(2)}) async-start(bf16[256,8,512]{2,0,1:T(8,128)(2,1)} %bitcast.100), calls=%async_computation.4 | async-start | bytes 4194304 | tf_op jit(solution)/shard_map/all_to_all | solution.py:392
  60.4 33.7 %collective-permute-start.1 = (bf16[128,512]{1,0:T(8,128)(2,1)S(1)}, bf16[128,512]{1,0:T(8,128)(2,1)S(1)}, u32[]{:S(2)}, u32[]{:S(2)}) collective-permute-start(bf16[128,512]{1,0:T(8,128)(2,1)S(1)} %bitcast.116), channel_id=1, source_target_pairs={{0,8},{1,9},{2,10},{3,11},{4,12},{5,13},{6,14},{7,15},{8,0},{9,1},... | collective-permute-start | bytes 393224 | tf_op jit(solution)/shard_map/ppermute | solution.py:368
  106.4 15.7 %copy-start.2 = (pred[512,8192]{0,1:T(8,128)(4,1)S(1)}, pred[512,8192]{0,1:T(8,128)(4,1)}, u32[]{:S(2)}) copy-start(pred[512,8192]{0,1:T(8,128)(4,1)} %iota_compare_fusion) | copy-start | bytes 12582916
  155.3 6.1 %collective-permute-start = (bf16[128,256]{1,0:T(8,128)(2,1)S(1)}, bf16[128,256]{1,0:T(8,128)(2,1)S(1)}, u32[]{:S(2)}, u32[]{:S(2)}) collective-permute-start(bf16[128,256]{1,0:T(8,128)(2,1)S(1)} %bitcast.117), channel_id=1, source_target_pairs={{0,8},{1,9},{2,10},{3,11},{4,12},{5,13},{6,14},{7,15},{8,0},{9,1},... | collective-permute-start | bytes 196616 | tf_op jit(solution)/shard_map/ppermute | solution.py:368
  162.2 82.8 %copy-start.1 = (bf16[64,1024]{1,0:T(8,128)(2,1)S(1)}, bf16[64,1024]{1,0:T(8,128)(2,1)}, u32[]{:S(2)}) copy-start(bf16[64,1024]{1,0:T(8,128)(2,1)} %param.11) | copy-start | bytes 393220
Sparse Core Ops, SparseCore 0:
  30.3 76.0 all-gather.1

commit v2 on v1

--- a/solution.py
+++ b/solution.py
@@ -5,8 +5,6 @@
 from jax.experimental.pallas import tpu as pltpu
 from jax.sharding import PartitionSpec as P
 
-HEADS = 16
-KV_HEADS = 8
 HEAD_DIM = 128
 MESH = pl.DeviceIdType.MESH
 F32 = jnp.float32
@@ -29,6 +27,24 @@
         self.left = self.at_x(self.xs[3])
         self.above = self.at_z(1)
         self.below = self.at_z(3)
+
+        self.y = self.yc // 2
+        self.core = lax.rem(self.blk, 2)
+        self.chip = self.blk // 2
+        self.up = self.at_y(1)
+        self.down = self.at_y(3)
+        self.partner = (self.head, self.blk + 1 - 2 * self.core)
+        self.across = (self.head, (1 - self.zh) * 8 + self.yc)
+
+    def at_y(self, step):
+        return (self.head, self.zh * 8 + lax.rem(self.y + step, 4) * 2 + self.core)
+
+    def plane(self, step, k):
+        z = lax.rem(self.z + step, 4)
+        return (lax.rem(z, 2) * 4 + self.xs[k], (z // 2) * 8 + self.yc)
+
+    def chip_at(self, dz, k):
+        return lax.rem(self.zh + dz, 2) * 4 + lax.rem(self.y + k, 4)
 
     def at_x(self, x):
         return (self.zl * 4 + x, self.blk)
@@ -100,6 +116,255 @@
     pltpu.make_async_copy(buf.at[0:7], buf.at[0:7], send_sem).wait()
 
 
+def columns(h, width):
+    return pl.ds(pl.multiple_of(h * width, width), width)
+
+
+SCALE = HEAD_DIM ** (-0.5) * 1.4426950408889634
+
+
+def attend_blocks(
+    p, q, k, v, hid_in, wo_hbm, kv, qbuf, hid, wo, qs, oa, peak, abuf,
+    sk, kv1, q1, h1, w1, w2, ysem, zrecv, csem, wown,
+):
+    own = p.blk
+    mine = pl.ds(pl.multiple_of(p.x * 32, 32), 32)
+
+    def rows_of(g):
+        return pl.ds(pl.multiple_of(g * 128 + p.x * 32, 32), 32)
+
+    kv_rows = pl.ds(pl.multiple_of(p.head * 64, 64), 64)
+
+    def send_kv(device):
+        h = device[0]
+        remote(k.at[:, columns(h, 128)], kv.at[own, kv_rows, 0:128], sk, kv1, device).start()
+        remote(v.at[:, columns(h, 128)], kv.at[own, kv_rows, 128:256], sk, kv1, device).start()
+
+    def send_rows(src, dst, sem, width, part, g, device):
+        at = columns(device[0], width)
+        remote(src.at[part * 32 : (part + 1) * 32, at], dst.at[rows_of(g), :], sk, sem, device).start()
+
+    near = 1 - 2 * p.zl + 4
+    for kx in range(4):
+        send_kv(p.plane(near, kx))
+        if kx:
+            send_kv(p.plane(0, kx))
+    for kx in range(4):
+        send_rows(q, qbuf, q1, 256, 0, 2, p.plane(1, kx))
+        send_rows(q, qbuf, q1, 256, 1, 1, p.plane(3, kx))
+        if kx:
+            send_rows(q, qbuf, q1, 256, 0, 0, p.plane(0, kx))
+            send_rows(q, qbuf, q1, 256, 1, 3, p.plane(0, kx))
+
+    def block(dz, kk, other=False):
+        core = 1 - p.core if other else p.core
+        return p.chip_at(dz, kk) * 2 + core
+
+    def piece(dz, kk, part):
+        return kv.at[block(dz, kk), part * 256 : (part + 1) * 256, 0:256]
+
+    def send_piece(dz, kk, part, sem, device):
+        remote(piece(dz, kk, part), piece(dz, kk, part), sk, sem, device).start()
+
+    def wait_piece(dz, kk, part, sem):
+        remote(piece(dz, kk, part), piece(dz, kk, part), sk, sem, p.up).wait_recv()
+
+    def share(dz, kk, sem):
+        ref = kv.at[block(dz, kk), :, 0:256]
+        remote(ref, ref, sk, sem, p.partner).start()
+
+    def wait_shared(dz, kk, sem):
+        ref = kv.at[block(dz, kk, True), :, 0:256]
+        remote(ref, ref, sk, sem, p.partner).wait_recv()
+
+    def send_both(dz):
+        i = 3 * dz
+        send_piece(dz, 0, 0, ysem.at[0, i], p.up)
+        send_piece(dz, 0, 1, ysem.at[1, i + 1], p.down)
+        send_piece(dz, 0, 1, ysem.at[0, i + 1], p.up)
+        send_piece(dz, 0, 0, ysem.at[1, i], p.down)
+
+    def forward(dz):
+        i = 3 * dz
+        wait_piece(dz, 3, 0, ysem.at[0, i])
+        send_piece(dz, 3, 0, ysem.at[0, i + 2], p.up)
+        wait_piece(dz, 1, 1, ysem.at[1, i + 1])
+        send_piece(dz, 1, 1, ysem.at[1, i + 2], p.down)
+
+    def near_done(dz):
+        i = 3 * dz
+        wait_piece(dz, 3, 1, ysem.at[0, i + 1])
+        share(dz, 3, csem.at[4 * dz + 3])
+        wait_piece(dz, 1, 0, ysem.at[1, i])
+        share(dz, 1, csem.at[4 * dz + 1])
+
+    def far_done(dz):
+        i = 3 * dz
+        wait_piece(dz, 2, 0, ysem.at[0, i + 2])
+        wait_piece(dz, 2, 1, ysem.at[1, i + 2])
+        share(dz, 2, csem.at[4 * dz + 2])
+
+    ref = kv.at[own, 0:448, 0:256]
+    remote(ref, ref, sk, kv1, p.up).wait_recv()
+    send_both(0)
+    for part in range(2):
+        send_piece(0, 0, part, zrecv.at[part], p.across)
+    share(0, 0, csem.at[0])
+    for kx in range(4):
+        send_rows(hid_in, hid, h1, 512, 0, 2, p.plane(1, kx))
+        send_rows(hid_in, hid, h1, 512, 1, 1, p.plane(3, kx))
+        if kx:
+            send_rows(hid_in, hid, h1, 512, 0, 0, p.plane(0, kx))
+            send_rows(hid_in, hid, h1, 512, 1, 3, p.plane(0, kx))
+
+    ref = qbuf.at[0:448]
+    remote(ref, ref, sk, q1, p.up).wait_recv()
+    same = 1 + p.zl
+    for r in range(2):
+        cols = slice(r * 128, (r + 1) * 128)
+        qs[r * 384 : r * 384 + 128] = qbuf[0:128, cols]
+        qs[r * 384 + 128 : r * 384 + 256] = qbuf[pl.ds(pl.multiple_of(same * 128, 128), 128), cols]
+        qs[r * 384 + 256 : r * 384 + 384] = qbuf[384:512, cols]
+        qs[768 + r * 128 : 896 + r * 128] = qbuf[pl.ds(pl.multiple_of((3 - same) * 128, 128), 128), cols]
+    oa[...] = jnp.zeros_like(oa)
+    peak[...] = jnp.full_like(peak, negative_fill)
+
+    def absorb(start, count, chip, row_pos):
+        rows = pl.ds(start, count)
+        keys = kv[pl.ds(chip * 2, 2), :, 0:128].reshape(1024, 128)
+        s = lax.dot_general(qs[rows], keys, (((1,), (1,)), ((), ())), preferred_element_type=F32)
+        if row_pos is not None:
+            i = lax.broadcasted_iota(jnp.int32, (count, 1), 0)
+            key_pos = chip * 1024 + lax.broadcasted_iota(jnp.int32, (count, 1024), 1)
+            s = jnp.where(key_pos <= row_pos(i), s, negative_fill)
+        old = peak[rows]
+        new = jnp.maximum(old, jnp.max(s, axis=1, keepdims=True))
+        peak[rows] = new
+        w = jnp.exp2((s - new[:, 0:1]) * SCALE).astype(BF16)
+        shrink = jnp.exp2((old - new) * SCALE)
+        values = kv[pl.ds(chip * 2, 2), :, 128:384].reshape(1024, 256)
+        part = jnp.dot(w, values, preferred_element_type=F32)
+        oa[rows, 0:128] = oa[rows, 0:128] * shrink + part[:, 0:128]
+        oa[rows, 128:256] = oa[rows, 128:256] * shrink + part[:, 128:256]
+
+    def spread(i):
+        return ((i & 96) << 1) + (i & 31)
+
+    def pos_a(i):
+        seg = i >> 7
+        shift = jnp.where(seg == 1, (1 - p.zl) * 288, p.zl * 256 + (seg >> 1) * 32)
+        return own * 512 + spread(i & 127) + shift
+
+    chip_b = (1 - p.zh) * 4 + p.y
+
+    def pos_b(i):
+        return (chip_b * 2 + p.core) * 512 + spread(i & 127) + (1 - p.zl) * 256 + p.zl * 32
+
+    def absorb_a(chip, masked):
+        def one(r, _):
+            absorb(pl.multiple_of(r * 384, 128), 384, chip, pos_a if masked else None)
+            return 0
+
+        lax.fori_loop(0, 2, one, 0)
+
+    def absorb_b(chip, masked):
+        absorb(768, 256, chip, pos_b if masked else None)
+
+    def seen(chip):
+        @pl.when(chip < p.chip)
+        def _():
+            absorb_a(chip, False)
+
+        @pl.when(chip < chip_b)
+        def _():
+            absorb_b(chip, False)
+
+    wait_shared(0, 0, csem.at[0])
+    absorb_a(p.chip, True)
+
+    @pl.when(p.chip < chip_b)
+    def _():
+        absorb_b(p.chip, False)
+
+    forward(0)
+    near_done(0)
+    for part in range(2):
+        wait_piece(1, 0, part, zrecv.at[part])
+    send_both(1)
+    share(1, 0, csem.at[4])
+    half = pl.ds(pl.multiple_of(p.core * 128, 128), 128)
+    for kx in range(4):
+        if kx:
+            device = p.plane(0, kx)
+            remote(
+                wo_hbm.at[half, columns(device[0], 512)], wo.at[p.head, p.core], sk, w1, device
+            ).start()
+        for part in range(2):
+            device = p.plane(1 + 2 * part, kx)
+            rows = pl.ds(pl.multiple_of(p.core * 128 + part * 64, 64), 64)
+            remote(
+                wo_hbm.at[rows, columns(device[0], 512)],
+                wo.at[p.head, p.core, part * 64 : (part + 1) * 64], sk, w1, device,
+            ).start()
+    wait_shared(0, 3, csem.at[3])
+    wait_shared(0, 1, csem.at[1])
+
+    def near_step(t, _):
+        seen(p.chip_at(0, 3 - 2 * t))
+        return 0
+
+    lax.fori_loop(0, 2, near_step, 0)
+    far_done(0)
+    forward(1)
+    wait_shared(1, 0, csem.at[4])
+    chip = p.chip_at(1, 0)
+
+    @pl.when(chip < p.chip)
+    def _():
+        absorb_a(chip, False)
+
+    absorb_b(chip, True)
+    near_done(1)
+    wait_shared(0, 2, csem.at[2])
+    wait_shared(1, 3, csem.at[7])
+    wait_shared(1, 1, csem.at[5])
+
+    def late_step(t, _):
+        @pl.when(t == 3)
+        def _():
+            far_done(1)
+            wait_shared(1, 2, csem.at[6])
+
+        seen(p.chip_at(jnp.minimum(t, 1), 2 + t - 3 * (t // 2)))
+        return 0
+
+    lax.fori_loop(0, 4, late_step, 0)
+
+    wown.wait()
+    ref = wo.at[0:7, 0]
+    remote(ref, ref, sk, w1, p.up).wait_recv()
+    ref = wo.at[:, p.core]
+    remote(ref, ref, sk, w2, p.partner).start()
+
+    for r in range(2):
+        a = (oa[r * 384 : (r + 1) * 384, 0:128] / oa[r * 384 : (r + 1) * 384, 128:256]).astype(BF16)
+        abuf[p.head, r, 0, 0:128] = a[0:128]
+        abuf[p.head, r, p.zl, pl.ds(pl.multiple_of((1 - p.zl) * 128, 128), 128)] = a[128:256]
+        abuf[p.head, r, 1, 128:256] = a[256:384]
+        b = (oa[768 + r * 128 : 896 + r * 128, 0:128] / oa[768 + r * 128 : 896 + r * 128, 128:256]).astype(BF16)
+        abuf[p.head, r, 1 - p.zl, pl.ds(pl.multiple_of(p.zl * 128, 128), 128)] = b
+
+    ref = hid.at[0:448]
+    remote(ref, ref, sk, h1, p.up).wait_recv()
+    ref = wo.at[:, 1 - p.core]
+    remote(ref, ref, sk, w2, p.partner).wait_recv()
+
+    for ref in (
+        qbuf.at[0:448], hid.at[0:448], kv.at[own, 0:448, 0:256], kv.at[0:15, :, 0:256], wo.at[0:7, 0], wo.at[:, p.core],
+    ):
+        pltpu.make_async_copy(ref, ref, sk).wait()
+
+
 NS1 = 2
 NS2 = 4
 NC = 8
@@ -108,18 +373,26 @@
 
 
 def block_kernel(
-    att, hid, gain, wo_hbm, gate_hbm, up_hbm, down_hbm, out,
-    abuf, rbuf, wo, wgu, wd, oacc, acc, xg, sq, inner,
+    q, k, v, hid_in, gain, wo_hbm, gate_hbm, up_hbm, down_hbm, out,
+    kv, qbuf, qs, oa, peak,
+    abuf, rbuf, hid, wo, wgu, wd, oacc, acc, xg, sq, inner,
     zs, zr, keep, m1s, m1r, m2s, m2r,
-    wsem, s1, r1, s2, r2, s3, zsem, m1sem, m2sem,
+    wsem, sk, kv1, q1, h1, w1, w2, ysem, zrecv, csem,
+    s1, r1, s2, r2, s3, zsem, m1sem, m2sem,
 ):
     p = Place()
     barrier = pltpu.get_barrier_semaphore()
-    for device in (p.right, p.left, p.above, p.below):
+    peers = [p.plane(0, kx) for kx in (1, 2, 3)]
+    peers += [p.plane(step, kx) for step in (1, 3) for kx in range(4)]
+    peers += [p.up, p.down, p.across, p.partner]
+    for device in peers:
         pl.semaphore_signal(barrier, inc=1, device_id=device, device_id_type=MESH)
 
     order = [p.here(0), p.other(0), p.here(3), p.here(1), p.here(2), p.other(3), p.other(1), p.other(2)]
-    wo_copy = pltpu.make_async_copy(wo_hbm, wo, wsem.at[16])
+    half = pl.ds(pl.multiple_of(p.core * 128, 128), 128)
+    wo_copy = pltpu.make_async_copy(
+        wo_hbm.at[half, columns(p.head, 512)], wo.at[p.head, p.core], wsem.at[16]
+    )
     wd_copy = pltpu.make_async_copy(down_hbm, wd, wsem.at[17])
 
     def gate_copy(h):
@@ -138,19 +411,26 @@
 
     me = p.here(0)
     c1 = 256 // NS1
-    for s in range(NS1):
-        for half in range(2):
-            abuf[me, s, half] = att[half * 256 : (half + 1) * 256, s * c1 : (s + 1) * c1]
-    pl.semaphore_wait(barrier, 4)
+    kv[:, :, 256:384] = jnp.ones((16, 512, 128), BF16)
+    kv_rows = pl.ds(pl.multiple_of(p.head * 64, 64), 64)
+    kv[p.blk, kv_rows, 0:128] = k[:, columns(p.head, 128)]
+    kv[p.blk, kv_rows, 128:256] = v[:, columns(p.head, 128)]
+    for part in range(2):
+        rows = pl.ds(pl.multiple_of(part * 384 + p.x * 32, 32), 32)
+        qbuf[rows, :] = q[part * 32 : (part + 1) * 32, columns(p.head, 256)]
+        hid[rows, :] = hid_in[part * 32 : (part + 1) * 32, columns(p.head, 512)]
+    pl.semaphore_wait(barrier, len(peers))
+    attend_blocks(
+        p, q, k, v, hid_in, wo_hbm, kv, qbuf, hid, wo, qs, oa, peak, abuf,
+        sk, kv1, q1, h1, w1, w2, ysem, zrecv, csem, wo_copy,
+    )
 
     def project(h, first):
-        if first:
-            wo_copy.wait()
         a = jnp.concatenate([abuf[h, s].reshape(512, c1) for s in range(NS1)], axis=1)
-        rows = pl.ds(pl.multiple_of(h * 256, 256), 256)
+        w = wo[h].reshape(256, 512)
         for n in range(2):
             cols = slice(n * 256, (n + 1) * 256)
-            part = jnp.dot(a, wo[rows, cols], preferred_element_type=F32)
+            part = jnp.dot(a, w[:, cols], preferred_element_type=F32)
             if first:
                 oacc[:, cols] = hid[:, cols].astype(F32) + part
             else:
@@ -281,19 +561,25 @@
     pltpu.make_async_copy(m2s, m2s, s3).wait()
 
 
-def feed_forward(att, hid, wo, gain, gate, up, down):
+def layer(q, k, v, hidden, gain, wo, gate, up, down):
     vmem = pl.BlockSpec(memory_space=pltpu.VMEM)
     hbm = pl.BlockSpec(memory_space=pl.ANY)
     dma = pltpu.SemaphoreType.DMA
     return pl.pallas_call(
         block_kernel,
         out_shape=jax.ShapeDtypeStruct((64, 4096), BF16),
-        in_specs=[vmem, vmem, vmem, hbm, hbm, hbm, hbm],
+        in_specs=[vmem, vmem, vmem, vmem, vmem, hbm, hbm, hbm, hbm],
         out_specs=vmem,
         scratch_shapes=[
+            pltpu.VMEM((16, 512, 384), BF16),
+            pltpu.VMEM((512, 256), BF16),
+            pltpu.VMEM((1024, 128), BF16),
+            pltpu.VMEM((1024, 256), F32),
+            pltpu.VMEM((1024, 128), F32),
             pltpu.VMEM((8, NS1, 2, 256, 256 // NS1), BF16),
             pltpu.VMEM((8, NS2, 2, 256, 512 // NS2), BF16),
-            pltpu.VMEM((2048, 512), BF16),
+            pltpu.VMEM((512, 512), BF16),
+            pltpu.VMEM((8, 2, 128, 512), BF16),
             pltpu.VMEM((4096, 2 * FFL), BF16),
             pltpu.VMEM((FFL, 4096), BF16),
             pltpu.VMEM((512, 512), F32),
@@ -310,6 +596,15 @@
             pltpu.VMEM((NC, 2, 2, 32, CW), BF16),
             dma((18,)),
             dma,
+            dma,
+            dma,
+            dma,
+            dma,
+            dma,
+            dma((2, 6)),
+            dma((2,)),
+            dma((8,)),
+            dma,
             dma((14, NS1)),
             dma,
             dma((14, NS2)),
@@ -321,54 +616,9 @@
         compiler_params=pltpu.CompilerParams(
             collective_id=1, has_side_effects=True, vmem_limit_bytes=62 * 1024 * 1024
         ),
-        cost_estimate=pl.CostEstimate(flops=12_500_000_000, bytes_accessed=24_000_000, transcendentals=0),
-        name="feed_forward",
-    )(att, hid, gain, wo, gate, up, down)
-
-
-def sent_together(arrays, axis, dim, along):
-    ends, at = ([], 0)
-    for a in arrays[:-1]:
-        at += a.shape[along]
-        ends.append(at)
-    both = jnp.concatenate(arrays, axis=along)
-    return tuple(jnp.split(lax.all_gather(both, axis, axis=dim, tiled=True), ends, axis=along))
-
-
-def absorb_rows(query_groups, query_pos, key_block, value_block, key_pos):
-    key_count = key_block.shape[0]
-    group_count = query_groups.shape[1]
-    head_size = query_groups.shape[3]
-    key_heads = key_block.reshape(key_count, group_count, head_size)
-    value_heads = value_block.reshape(key_count, group_count, head_size)
-    scores = jnp.einsum(
-        "qgrd,kgd->grqk", query_groups, key_heads, preferred_element_type=jnp.float32
-    ) * head_size ** (-0.5)
-    visible = key_pos[None, :] <= query_pos[:, None]
-    new_peak = jnp.max(jnp.where(visible, scores, negative_fill), axis=-1)
-    exp_scores = jnp.where(visible, jnp.exp(scores - new_peak[..., None]), 0.0)
-    new_total = jnp.sum(exp_scores, axis=-1)
-    products = jnp.einsum(
-        "grqk,kgd->grqd",
-        exp_scores.astype(jnp.bfloat16),
-        value_heads,
-        preferred_element_type=jnp.float32,
-    )
-    return new_total, products
-
-
-def regroup(rows):
-    width = rows.shape[1]
-    zl = lax.axis_index("head") // 4
-    parts = rows.reshape(2, 4, 2, 32, width)
-    own = jnp.where(zl == 0, parts[0], parts[1])
-    other = jnp.where(zl == 0, parts[1], parts[0])
-    gives = jnp.where(zl == 0, other[:, 0], other[:, 1]).reshape(128, width)
-    keeps = jnp.where(zl == 0, other[:, 1], other[:, 0]).reshape(128, width)
-    gets = lax.ppermute(gives, "blk", [(b, (b + 8) % 16) for b in range(16)])
-    upper = jnp.where(zl == 0, keeps, gets)
-    lower = jnp.where(zl == 0, gets, keeps)
-    return jnp.concatenate([own[:, 0].reshape(128, width), upper, lower, own[:, 1].reshape(128, width)], axis=0)
+        cost_estimate=pl.CostEstimate(flops=16_500_000_000, bytes_accessed=24_000_000, transcendentals=0),
+        name="layer",
+    )(q, k, v, hidden, gain, wo, gate, up, down)
 
 
 def local(
@@ -382,34 +632,10 @@
     up_weight,
     down_weight,
 ):
-    own_block = lax.axis_index("blk")
-    query_local, key_local, value_local = (
-        lax.all_to_all(queries, "head", split_axis=1, concat_axis=0, tiled=True),
-        lax.all_to_all(key_states, "head", split_axis=1, concat_axis=0, tiled=True),
-        lax.all_to_all(value_states, "head", split_axis=1, concat_axis=0, tiled=True),
+    return layer(
+        queries, key_states, value_states, hidden_in, norm_gain.reshape(32, 128),
+        out_weight, gate_weight, up_weight, down_weight,
     )
-    hidden_local = lax.all_to_all(hidden_in, "head", split_axis=1, concat_axis=0, tiled=True)
-    wo = lax.all_to_all(out_weight, "head", split_axis=1, concat_axis=0, tiled=True)
-    block_rows = query_local.shape[0]
-    query_width = query_local.shape[1]
-    key_width = key_local.shape[1]
-    group_count = key_width // HEAD_DIM
-    group_ratio = HEADS // KV_HEADS
-    local_index = jnp.arange(block_rows, dtype=jnp.int32)
-    query_pos = own_block * block_rows + local_index
-    query_groups = query_local.reshape(block_rows, group_count, group_ratio, HEAD_DIM)
-    key_block, value_block = sent_together((key_local, value_local), "blk", 0, 1)
-    key_pos = jnp.arange(key_block.shape[0], dtype=jnp.int32)
-    row_total, weighted = absorb_rows(query_groups, query_pos, key_block, value_block, key_pos)
-    attended = (
-        (weighted / row_total[..., None])
-        .transpose(2, 0, 1, 3)
-        .reshape(block_rows, query_width)
-        .astype(jnp.bfloat16)
-    )
-    att = regroup(attended)
-    hid = regroup(hidden_local)
-    return feed_forward(att, hid, wo, norm_gain.reshape(4 * 8, 128), gate_weight, up_weight, down_weight)
 
 
 def solution(mesh):

time: 254 us -> 132 us (0.52)
  waiting for transfers between devices: 57.2 us -> 0 us
  Pallas kernels: 81 us -> 130 us
  matrix products: 33.7 us -> 0 us
  starting transfers between devices: 23 us -> 0 us
  other arithmetic: 22.8 us -> 0 us
  between operations: 13.5 us -> 0.01 us
  local copies, waits for them, and re-layouts: 11.6 us -> 1.87 us
  blocking collectives: 9.1 us -> 0 us
    pallas_call x1, Pallas kernels: 81 us -> 130 us  [layer(): pl.pallas_call(block_kernel, out_shape=jax.ShapeDtypeStruct((64, 4096), B...]
    ppermute x2 -> x0, waiting for transfers between devices: 34.8 us -> none  [regroup(): gets = lax.ppermute(gives, 'blk', [(b, (b + 8) % 16) for b in range(16)])]
    dot_general x2 -> x0, matrix products: 33.7 us -> none  [the longest x1 18 us: absorb_rows(): jnp.einsum('grqk,kgd->grqd', exp_scores.astype(jnp.bfloat16), value_heads...]
    all_to_all x4 -> x0, starting transfers between devices: 18.2 us -> none  [the longest x1 5.65 us: local(): lax.all_to_all(key_states, 'head', split_axis=1, concat_axis=0, tiled=True)]
    reduce_sum x1 -> x0, other arithmetic: 14.9 us -> none  [absorb_rows(): new_total = jnp.sum(exp_scores, axis=-1)]
    all_gather x1 -> x0, waiting for transfers between devices: 11.4 us -> none  [sent_together(): lax.all_gather(both, axis, axis=dim, tiled=True)]
    all_to_all x4 -> x0, waiting for transfers between devices: 10.9 us -> none  [the longest x1 5.61 us: local(): lax.all_to_all(key_states, 'head', split_axis=1, concat_axis=0, tiled=True)]
    all_to_all x1 -> x0, blocking collectives: 9.1 us -> none  [local(): lax.all_to_all(value_states, 'head', split_axis=1, concat_axis=0, tiled=T...]
  transfers between devices with their start and end apart: 7 -> 0, of which waited for: 5 -> 0; matrix products, arithmetic and copies ran while one was open for 25% -> 0% of each run, Pallas kernels for 0% -> 0%
where the time goes in v2:
time: 132 us
  Pallas kernels  130 us (98%)
  local copies, waits for them, and re-layouts  1.87 us (1%)
    pallas_call x1, Pallas kernels, layer(): pl.pallas_call(block_kernel, out_shape=jax.ShapeDtypeStruct((64, 4096), B...  130 us

profile of v2, /device:TPU:24, one launch (start us, length us, event | category | flops | bytes accessed | tf_op | source)
XLA Modules:
  0.0 132.0 jit_solution(6589646264189791583)
XLA Ops:
  0.0 130.1 %layer.1 = bf16[64,4096]{1,0:T(8,128)(2,1)} custom-call(bf16[64,2048]{1,0:T(8,128)(2,1)} %q.1, bf16[64,1024]{1,0:T(8,128)(2,1)} %k.1, bf16[64,1024]{1,0:T(8,128)(2,1)} %v.1, bf16[64,4096]{1,0:T(8,128)(2,1)} %hid_in.1, f32[32,128]{1,0:T(8,128)} %bitcast.1, bf16[256,4096]{1,0:T(8,128)(2,1)} %wo_hbm.1, bf16[4096,896]{1,0:T(8,128)(2,1)} %gate_hbm.1, ...), custom_call_target="tpu_custom_call" | custom-call | flops 16499999744 | bytes 24000000 | tf_op jit(solution)/shard_map/layer/pallas_call | solution.py:568
  130.1 1.9 %copy.11 = bf16[64,4096]{1,0:T(8,128)(2,1)} copy(bf16[64,4096]{1,0:T(8,128)(2,1)} %layer.1) | data formatting | bytes 1048576

commit v3 on v2

--- a/solution.py
+++ b/solution.py
@@ -135,10 +135,10 @@
 
     kv_rows = pl.ds(pl.multiple_of(p.head * 64, 64), 64)
 
-    def send_kv(device):
+    def send_kv(device, sem):
         h = device[0]
-        remote(k.at[:, columns(h, 128)], kv.at[own, kv_rows, 0:128], sk, kv1, device).start()
-        remote(v.at[:, columns(h, 128)], kv.at[own, kv_rows, 128:256], sk, kv1, device).start()
+        remote(k.at[:, columns(h, 128)], kv.at[own, kv_rows, 0:128], sk, sem, device).start()
+        remote(v.at[:, columns(h, 128)], kv.at[own, kv_rows, 128:256], sk, sem, device).start()
 
     def send_rows(src, dst, sem, width, part, g, device):
         at = columns(device[0], width)
@@ -146,9 +146,9 @@
 
     near = 1 - 2 * p.zl + 4
     for kx in range(4):
-        send_kv(p.plane(near, kx))
+        send_kv(p.plane(near, kx), kv1.at[1])
         if kx:
-            send_kv(p.plane(0, kx))
+            send_kv(p.plane(0, kx), kv1.at[0])
     for kx in range(4):
         send_rows(q, qbuf, q1, 256, 0, 2, p.plane(1, kx))
         send_rows(q, qbuf, q1, 256, 1, 1, p.plane(3, kx))
@@ -204,11 +204,16 @@
         wait_piece(dz, 2, 1, ysem.at[1, i + 2])
         share(dz, 2, csem.at[4 * dz + 2])
 
-    ref = kv.at[own, 0:448, 0:256]
-    remote(ref, ref, sk, kv1, p.up).wait_recv()
-    send_both(0)
-    for part in range(2):
-        send_piece(0, 0, part, zrecv.at[part], p.across)
+    def own_rows(part):
+        return kv.at[own, pl.ds(pl.multiple_of(part * 256, 256), 256), 0:256]
+
+    for order, (part, count) in enumerate(((p.zl, 192), (1 - p.zl, 256))):
+        ref = kv.at[own, 0:count, 0:256]
+        remote(ref, ref, sk, kv1.at[order], p.up).wait_recv()
+        ref = own_rows(part)
+        remote(ref, ref, sk, ysem.at[0, part], p.up).start()
+        remote(ref, ref, sk, ysem.at[1, part], p.down).start()
+        remote(ref, ref, sk, zrecv.at[part], p.across).start()
     share(0, 0, csem.at[0])
     for kx in range(4):
         send_rows(hid_in, hid, h1, 512, 0, 2, p.plane(1, kx))
@@ -229,29 +234,46 @@
     oa[...] = jnp.zeros_like(oa)
     peak[...] = jnp.full_like(peak, negative_fill)
 
-    def absorb(start, count, chip, row_pos):
-        rows = pl.ds(start, count)
+    def absorb(start, count, sub, chip, row_pos):
         keys = kv[pl.ds(chip * 2, 2), :, 0:128].reshape(1024, 128)
-        s = lax.dot_general(qs[rows], keys, (((1,), (1,)), ((), ())), preferred_element_type=F32)
-        if row_pos is not None:
-            i = lax.broadcasted_iota(jnp.int32, (count, 1), 0)
-            key_pos = chip * 1024 + lax.broadcasted_iota(jnp.int32, (count, 1024), 1)
-            s = jnp.where(key_pos <= row_pos(i), s, negative_fill)
-        old = peak[rows]
-        new = jnp.maximum(old, jnp.max(s, axis=1, keepdims=True))
-        peak[rows] = new
-        w = jnp.exp2((s - new[:, 0:1]) * SCALE).astype(BF16)
-        shrink = jnp.exp2((old - new) * SCALE)
         values = kv[pl.ds(chip * 2, 2), :, 128:384].reshape(1024, 256)
-        part = jnp.dot(w, values, preferred_element_type=F32)
-        oa[rows, 0:128] = oa[rows, 0:128] * shrink + part[:, 0:128]
-        oa[rows, 128:256] = oa[rows, 128:256] * shrink + part[:, 128:256]
+        tiles = [slice(start + at, start + at + sub) for at in range(0, count, sub)]
+        asked = [qs[rows] for rows in tiles]
+        olds = [peak[rows] for rows in tiles]
+        sums = [oa[rows] for rows in tiles]
+
+        def score(t):
+            s = lax.dot_general(asked[t], keys, (((1,), (1,)), ((), ())), preferred_element_type=F32)
+            if row_pos is not None:
+                i = t * sub + lax.broadcasted_iota(jnp.int32, (sub, 1), 0)
+                key_pos = chip * 1024 + lax.broadcasted_iota(jnp.int32, (sub, 1024), 1)
+                s = jnp.where(key_pos <= row_pos(i), s, negative_fill)
+            return [s[:, at : at + 128] for at in range(0, 1024, 128)]
+
+        news, ends = [], []
+        coming = score(0)
+        for t, old in enumerate(olds):
+            s = coming
+            top = s[0]
+            for piece in s[1:]:
+                top = jnp.maximum(top, piece)
+            if t + 1 < len(tiles):
+                coming = score(t + 1)
+            new = jnp.maximum(old, jnp.max(top, axis=1, keepdims=True))
+            w = jnp.concatenate([jnp.exp2((piece - new) * SCALE).astype(BF16) for piece in s], axis=1)
+            shrink = jnp.exp2((old - new) * SCALE)
+            part = jnp.dot(w, values, preferred_element_type=F32)
+            news.append(new)
+            ends.append(sums[t] * jnp.concatenate([shrink, shrink], axis=1) + part)
+        for rows, new, end in zip(tiles, news, ends):
+            peak[rows] = new
+            oa[rows] = end
 
     def spread(i):
         return ((i & 96) << 1) + (i & 31)
 
     def pos_a(i):
-        seg = i >> 7
+        seg = lax.rem(i >> 7, 3)
         shift = jnp.where(seg == 1, (1 - p.zl) * 288, p.zl * 256 + (seg >> 1) * 32)
         return own * 512 + spread(i & 127) + shift
 
@@ -261,14 +283,10 @@
         return (chip_b * 2 + p.core) * 512 + spread(i & 127) + (1 - p.zl) * 256 + p.zl * 32
 
     def absorb_a(chip, masked):
-        def one(r, _):
-            absorb(pl.multiple_of(r * 384, 128), 384, chip, pos_a if masked else None)
-            return 0
-
-        lax.fori_loop(0, 2, one, 0)
+        absorb(0, 768, 256, chip, pos_a if masked else None)
 
     def absorb_b(chip, masked):
-        absorb(768, 256, chip, pos_b if masked else None)
+        absorb(768, 256, 128, chip, pos_b if masked else None)
 
     def seen(chip):
         @pl.when(chip < p.chip)
@@ -457,17 +475,12 @@
         else:
             sq[...] += total
         rows = pl.ds(pl.multiple_of(h * 512, 512), 512)
-
-        def tile(n, _):
-            cols = pl.ds(pl.multiple_of(n * 256, 256), 256)
-            part = jnp.dot(xg[...], wgu[rows, cols], preferred_element_type=F32)
+        for m in range(0, 512, 256):
+            part = jnp.dot(xg[m : m + 256], wgu[rows, :], preferred_element_type=F32)
             if first:
-                acc[:, cols] = part
+                acc[m : m + 256] = part
             else:
-                acc[:, cols] += part
-            return 0
-
-        lax.fori_loop(0, 7, tile, 0)
+                acc[m : m + 256] += part
 
     gather_rows(p, rbuf, s2, r2, NS2, expand)
 
@@ -491,14 +504,13 @@
         remote(zr.at[c, side], zr.at[c, side], s3, zsem.at[side, c], p.right).wait_recv()
 
     def reduce_down(c, _):
-        for n in range(2):
-            at = slice(n * 256, (n + 1) * 256)
-            cols = pl.ds(pl.multiple_of(c * CW + n * 256, 256), 256)
-            part = jnp.dot(inner[...], wd[:, cols], preferred_element_type=F32)
-            keep[c, 0, :, at] = part[0:128]
-            zs[c, 0, :, at] = part[128:256].astype(BF16)
-            zs[c, 1, :, at] = part[256:384].astype(BF16)
-            keep[c, 1, :, at] = part[384:512]
+        cols = pl.ds(pl.multiple_of(c * CW, CW), CW)
+        low = jnp.dot(inner[0:256], wd[:, cols], preferred_element_type=F32)
+        high = jnp.dot(inner[256:512], wd[:, cols], preferred_element_type=F32)
+        keep[c, 0] = low[0:128]
+        zs[c, 0] = low[128:256].astype(BF16)
+        zs[c, 1] = high[0:128].astype(BF16)
+        keep[c, 1] = high[128:256]
         z_copy(c, 0).start()
         z_copy(c, 1).start()
         return 0
@@ -596,7 +608,7 @@
             pltpu.VMEM((NC, 2, 2, 32, CW), BF16),
             dma((18,)),
             dma,
-            dma,
+            dma((2,)),
             dma,
             dma,
             dma,

time: 132 us -> 122 us (0.924)
  Pallas kernels: 130 us -> 120 us
    pallas_call x1, Pallas kernels: 130 us -> 120 us  [layer(): pl.pallas_call(block_kernel, out_shape=jax.ShapeDtypeStruct((64, 4096), B...]
where the time goes in v3:
time: 122 us
  Pallas kernels  120 us (98%)
  local copies, waits for them, and re-layouts  1.87 us (2%)
    pallas_call x1, Pallas kernels, layer(): pl.pallas_call(block_kernel, out_shape=jax.ShapeDtypeStruct((64, 4096), B...  120 us

profile of v3, /device:TPU:24, one launch (start us, length us, event | category | flops | bytes accessed | tf_op | source)
XLA Modules:
  0.0 122.2 jit_solution(7664117023415753696)
XLA Ops:
  0.0 120.3 %layer.1 = bf16[64,4096]{1,0:T(8,128)(2,1)} custom-call(bf16[64,2048]{1,0:T(8,128)(2,1)} %q.1, bf16[64,1024]{1,0:T(8,128)(2,1)} %k.1, bf16[64,1024]{1,0:T(8,128)(2,1)} %v.1, bf16[64,4096]{1,0:T(8,128)(2,1)} %hid_in.1, f32[32,128]{1,0:T(8,128)} %bitcast.1, bf16[256,4096]{1,0:T(8,128)(2,1)} %wo_hbm.1, bf16[4096,896]{1,0:T(8,128)(2,1)} %gate_hbm.1, ...), custom_call_target="tpu_custom_call" | custom-call | flops 16499999744 | bytes 24000000 | tf_op jit(solution)/shard_map/layer/pallas_call | solution.py:580
  120.3 1.9 %copy.11 = bf16[64,4096]{1,0:T(8,128)(2,1)} copy(bf16[64,4096]{1,0:T(8,128)(2,1)} %layer.1) | data formatting | bytes 1048576

commit v4 on v3

--- a/solution.py
+++ b/solution.py
@@ -67,12 +67,14 @@
     )
 
 
-def gather_rows(p, buf, send_sem, recv, steps, compute):
+def gather_rows(p, buf, batch, send_sem, recv, steps, compute):
     def send(h, s, half, to_half, kind, device):
-        remote(buf.at[h, s, half], buf.at[h, s, to_half], send_sem, recv.at[kind, s], device).start()
+        src, dst = buf.at[h, s, batch, half], buf.at[h, s, batch, to_half]
+        remote(src, dst, send_sem, recv.at[kind, s, batch], device).start()
 
     def wait(h, s, half, kind):
-        remote(buf.at[h, s, half], buf.at[h, s, half], send_sem, recv.at[kind, s], p.right).wait_recv()
+        ref = buf.at[h, s, batch, half]
+        remote(ref, ref, send_sem, recv.at[kind, s, batch], p.right).wait_recv()
 
     me, left, right, far = p.here(0), p.here(3), p.here(1), p.here(2)
     for s in range(steps):
@@ -80,10 +82,13 @@
         send(me, s, 1, 1, 4, p.left)
         send(me, s, 0, 1, 6, p.above)
         send(me, s, 1, 0, 10, p.below)
+    yield
     for s in range(steps):
         send(me, s, 1, 1, 1, p.right)
         send(me, s, 0, 0, 3, p.left)
+    yield
     compute(me, True)
+    yield
     for s in range(steps):
         wait(left, s, 0, 0)
         send(left, s, 0, 0, 2, p.right)
@@ -91,29 +96,39 @@
         wait(right, s, 1, 4)
         send(right, s, 1, 1, 5, p.left)
         send(right, s, 1, 0, 12, p.below)
+    yield
     for s in range(steps):
         wait(p.other(0), s, 1, 6)
         wait(p.other(0), s, 0, 10)
     compute(p.other(0), False)
+    yield
     for s in range(steps):
         wait(left, s, 1, 1)
         send(left, s, 1, 0, 11, p.below)
         wait(right, s, 0, 3)
         send(right, s, 0, 1, 8, p.above)
+    yield
     compute(left, False)
     compute(right, False)
+    yield
     for s in range(steps):
         wait(far, s, 0, 2)
         send(far, s, 0, 1, 9, p.above)
         wait(far, s, 1, 5)
         send(far, s, 1, 0, 13, p.below)
+    yield
     compute(far, False)
     for k, up, down in ((3, 7, 11), (1, 8, 12), (2, 9, 13)):
+        yield
         for s in range(steps):
             wait(p.other(k), s, 1, up)
             wait(p.other(k), s, 0, down)
         compute(p.other(k), False)
-    pltpu.make_async_copy(buf.at[0:7], buf.at[0:7], send_sem).wait()
+
+
+def advance(stages, count):
+    for _ in range(count):
+        next(stages, None)
 
 
 def columns(h, width):
@@ -121,6 +136,10 @@
 
 
 SCALE = HEAD_DIM ** (-0.5) * 1.4426950408889634
+
+
+def batch_rows(group, b):
+    return jnp.concatenate([group[at + b * 16 : at + b * 16 + 16] for at in range(0, 128, 32)], axis=0)
 
 
 def attend_blocks(
@@ -350,6 +369,11 @@
     def late_step(t, _):
         @pl.when(t == 3)
         def _():
+            wown.wait()
+            ref = wo.at[0:7, 0]
+            remote(ref, ref, sk, w1, p.up).wait_recv()
+            ref = wo.at[:, p.core]
+            remote(ref, ref, sk, w2, p.partner).start()
             far_done(1)
             wait_shared(1, 2, csem.at[6])
 
@@ -358,19 +382,15 @@
 
     lax.fori_loop(0, 4, late_step, 0)
 
-    wown.wait()
-    ref = wo.at[0:7, 0]
-    remote(ref, ref, sk, w1, p.up).wait_recv()
-    ref = wo.at[:, p.core]
-    remote(ref, ref, sk, w2, p.partner).start()
-
     for r in range(2):
+        cols = slice(r * 128, (r + 1) * 128)
         a = (oa[r * 384 : (r + 1) * 384, 0:128] / oa[r * 384 : (r + 1) * 384, 128:256]).astype(BF16)
-        abuf[p.head, r, 0, 0:128] = a[0:128]
-        abuf[p.head, r, p.zl, pl.ds(pl.multiple_of((1 - p.zl) * 128, 128), 128)] = a[128:256]
-        abuf[p.head, r, 1, 128:256] = a[256:384]
-        b = (oa[768 + r * 128 : 896 + r * 128, 0:128] / oa[768 + r * 128 : 896 + r * 128, 128:256]).astype(BF16)
-        abuf[p.head, r, 1 - p.zl, pl.ds(pl.multiple_of(p.zl * 128, 128), 128)] = b
+        o = (oa[768 + r * 128 : 896 + r * 128, 0:128] / oa[768 + r * 128 : 896 + r * 128, 128:256]).astype(BF16)
+        for b in range(2):
+            abuf[p.head, 0, b, 0, 0:64, cols] = batch_rows(a[0:128], b)
+            abuf[p.head, 0, b, p.zl, pl.ds(pl.multiple_of((1 - p.zl) * 64, 64), 64), cols] = batch_rows(a[128:256], b)
+            abuf[p.head, 0, b, 1, 64:128, cols] = batch_rows(a[256:384], b)
+            abuf[p.head, 0, b, 1 - p.zl, pl.ds(pl.multiple_of(p.zl * 64, 64), 64), cols] = batch_rows(o, b)
 
     ref = hid.at[0:448]
     remote(ref, ref, sk, h1, p.up).wait_recv()
@@ -383,19 +403,19 @@
         pltpu.make_async_copy(ref, ref, sk).wait()
 
 
-NS1 = 2
-NS2 = 4
+NS1 = 1
+NS2 = 2
 NC = 8
 CW = 512
 FFL = 896
 
 
 def block_kernel(
-    q, k, v, hid_in, gain, wo_hbm, gate_hbm, up_hbm, down_hbm, out,
-    kv, qbuf, qs, oa, peak,
+    q_hbm, k_hbm, v_hbm, hid_hbm, gain_hbm, wo_hbm, gate_hbm, up_hbm, down_hbm, out,
+    q, k, v, hid_in, gain, kv, qbuf, qs, oa, peak,
     abuf, rbuf, hid, wo, wgu, wd, oacc, acc, xg, sq, inner,
     zs, zr, keep, m1s, m1r, m2s, m2r,
-    wsem, sk, kv1, q1, h1, w1, w2, ysem, zrecv, csem,
+    insem, wsem, sk, kv1, q1, h1, w1, w2, ysem, zrecv, csem,
     s1, r1, s2, r2, s3, zsem, m1sem, m2sem,
 ):
     p = Place()
@@ -405,6 +425,12 @@
     peers += [p.up, p.down, p.across, p.partner]
     for device in peers:
         pl.semaphore_signal(barrier, inc=1, device_id=device, device_id_type=MESH)
+    loads = [
+        pltpu.make_async_copy(src, dst, insem.at[i])
+        for i, (src, dst) in enumerate(((k_hbm, k), (v_hbm, v), (q_hbm, q), (hid_hbm, hid_in), (gain_hbm, gain)))
+    ]
+    for load in loads:
+        load.start()
 
     order = [p.here(0), p.other(0), p.here(3), p.here(1), p.here(2), p.other(3), p.other(1), p.other(2)]
     half = pl.ds(pl.multiple_of(p.core * 128, 128), 128)
@@ -428,9 +454,10 @@
     wd_copy.start()
 
     me = p.here(0)
-    c1 = 256 // NS1
     kv[:, :, 256:384] = jnp.ones((16, 512, 128), BF16)
     kv_rows = pl.ds(pl.multiple_of(p.head * 64, 64), 64)
+    for load in loads:
+        load.wait()
     kv[p.blk, kv_rows, 0:128] = k[:, columns(p.head, 128)]
     kv[p.blk, kv_rows, 128:256] = v[:, columns(p.head, 128)]
     for part in range(2):
@@ -443,134 +470,173 @@
         sk, kv1, q1, h1, w1, w2, ysem, zrecv, csem, wo_copy,
     )
 
-    def project(h, first):
-        a = jnp.concatenate([abuf[h, s].reshape(512, c1) for s in range(NS1)], axis=1)
-        w = wo[h].reshape(256, 512)
-        for n in range(2):
-            cols = slice(n * 256, (n + 1) * 256)
-            part = jnp.dot(a, w[:, cols], preferred_element_type=F32)
+    c2 = 512 // NS2
+
+    def project(b):
+        rows = slice(b * 256, (b + 1) * 256)
+
+        def add(h, first):
+            part = jnp.dot(abuf[h, 0, b].reshape(256, 256), wo[h].reshape(256, 512), preferred_element_type=F32)
             if first:
-                oacc[:, cols] = hid[:, cols].astype(F32) + part
+                held = jnp.concatenate([batch_rows(hid[g * 128 : (g + 1) * 128], b) for g in range(4)], axis=0)
+                oacc[rows] = held.astype(F32) + part
             else:
-                oacc[:, cols] += part
-
-    gather_rows(p, abuf, s1, r1, NS1, project)
-
-    c2 = 512 // NS2
-    for s in range(NS2):
-        for half in range(2):
-            rbuf[me, s, half] = oacc[half * 256 : (half + 1) * 256, s * c2 : (s + 1) * c2].astype(BF16)
-
-    def expand(h, first):
-        gate_copy(h).wait()
-        up_copy(h).wait()
-        total = None
+                oacc[rows] += part
+
+        return add
+
+    def residual(b):
         for s in range(NS2):
-            r = rbuf[h, s].reshape(512, c2).astype(F32)
-            g = gain[pl.ds(h * NS2 + s, 1), :]
-            xg[:, s * c2 : (s + 1) * c2] = (r * g).astype(BF16)
-            total = r * r if total is None else total + r * r
-        if first:
-            sq[...] = total
-        else:
-            sq[...] += total
-        rows = pl.ds(pl.multiple_of(h * 512, 512), 512)
-        for m in range(0, 512, 256):
-            part = jnp.dot(xg[m : m + 256], wgu[rows, :], preferred_element_type=F32)
+            for half in range(2):
+                at = b * 256 + half * 128
+                rbuf[me, s, b, half] = oacc[at : at + 128, s * c2 : (s + 1) * c2].astype(BF16)
+
+    def expand(b):
+        out_rows = slice(b * 256, (b + 1) * 256)
+
+        def add(h, first):
+            if b == 0:
+                gate_copy(h).wait()
+                up_copy(h).wait()
+            total = None
+            for s in range(NS2):
+                r = rbuf[h, s, b].reshape(256, c2).astype(F32)
+                for j in range(c2 // 128):
+                    piece = r[:, j * 128 : (j + 1) * 128]
+                    g = gain[pl.ds(h * 4 + s * (c2 // 128) + j, 1), :]
+                    at = s * c2 + j * 128
+                    xg[b, :, at : at + 128] = (piece * g).astype(BF16)
+                    total = piece * piece if total is None else total + piece * piece
+            rows = pl.ds(pl.multiple_of(h * 512, 512), 512)
+            part = jnp.dot(xg[b], wgu[rows, :], preferred_element_type=F32)
             if first:
-                acc[m : m + 256] = part
+                sq[out_rows] = total
+                acc[out_rows] = part
             else:
-                acc[m : m + 256] += part
-
-    gather_rows(p, rbuf, s2, r2, NS2, expand)
-
-    scale = lax.rsqrt(jnp.sum(sq[...], axis=1, keepdims=True) * (1.0 / 4096.0) + 1e-5)
-    sq[...] = jnp.broadcast_to(scale, (512, 128))
-
-    def activate(j, _):
-        at = pl.multiple_of(j * 128, 128)
-        u = acc[:, pl.ds(at, 128)] * sq[...]
-        v = acc[:, pl.ds(pl.multiple_of(at + FFL, 128), 128)] * sq[...]
-        inner[:, pl.ds(at, 128)] = (u / (1.0 + jnp.exp(-u)) * v).astype(BF16)
-        return 0
-
-    lax.fori_loop(0, 7, activate, 0)
-
-    def z_copy(c, side):
-        device = p.above if side == 0 else p.below
-        return remote(zs.at[c, side], zr.at[c, 1 - side], s3, zsem.at[1 - side, c], device)
-
-    def z_wait(c, side):
-        remote(zr.at[c, side], zr.at[c, side], s3, zsem.at[side, c], p.right).wait_recv()
-
-    def reduce_down(c, _):
-        cols = pl.ds(pl.multiple_of(c * CW, CW), CW)
-        low = jnp.dot(inner[0:256], wd[:, cols], preferred_element_type=F32)
-        high = jnp.dot(inner[256:512], wd[:, cols], preferred_element_type=F32)
-        keep[c, 0] = low[0:128]
-        zs[c, 0] = low[128:256].astype(BF16)
-        zs[c, 1] = high[0:128].astype(BF16)
-        keep[c, 1] = high[128:256]
-        z_copy(c, 0).start()
-        z_copy(c, 1).start()
-        return 0
-
+                sq[out_rows] += total
+                acc[out_rows] += part
+
+        return add
+
+    def activate(b):
+        rows = slice(b * 256, (b + 1) * 256)
+        scale = lax.rsqrt(jnp.sum(sq[rows], axis=1, keepdims=True) * (1.0 / 4096.0) + 1e-5)
+        sq[rows] = jnp.broadcast_to(scale, (256, 128))
+
+        def tile(j, _):
+            at = pl.multiple_of(j * 128, 128)
+            u = acc[rows, pl.ds(at, 128)] * sq[rows]
+            v = acc[rows, pl.ds(pl.multiple_of(at + FFL, 128), 128)] * sq[rows]
+            inner[rows, pl.ds(at, 128)] = (u / (1.0 + jnp.exp(-u)) * v).astype(BF16)
+            return 0
+
+        lax.fori_loop(0, 7, tile, 0)
+
+    def reduce_down(b):
+        def one(c, _):
+            cols = pl.ds(pl.multiple_of(c * CW, CW), CW)
+            part = jnp.dot(inner[b * 256 : (b + 1) * 256], wd[:, cols], preferred_element_type=F32)
+            keep[b, c, 0] = part[0:64]
+            zs[b, c, 0] = part[64:128].astype(BF16)
+            zs[b, c, 1] = part[128:192].astype(BF16)
+            keep[b, c, 1] = part[192:256]
+            remote(zs.at[b, c, 0], zr.at[b, c, 1], s3, zsem.at[b, 1, c], p.above).start()
+            remote(zs.at[b, c, 1], zr.at[b, c, 0], s3, zsem.at[b, 0, c], p.below).start()
+            return 0
+
+        lax.fori_loop(0, NC, one, 0)
+
+    def slot(k):
+        return pl.ds(pl.multiple_of(p.xs[k] * 16, 16), 16)
+
+    def m1_copy(b, c, side):
+        device = p.right if side == 0 else p.left
+        return remote(m1s.at[b, c, side], m1r.at[b, c, side], s3, m1sem.at[b, side, c], device)
+
+    def m2_copy(b, c, side):
+        device = p.right if side == 0 else p.left
+        return remote(m2s.at[b, c, side], m2r.at[b, c, side], s3, m2sem.at[b, side, c], device)
+
+    def finish(b):
+        def one(t, _):
+            @pl.when(t < NC)
+            def _():
+                c = t
+                for side in range(2):
+                    ref = zr.at[b, c, side]
+                    remote(ref, ref, s3, zsem.at[b, side, c], p.right).wait_recv()
+                    keep[b, c, side] += zr[b, c, side].astype(F32)
+                    m1s[b, c, side] = keep[b, c, side, slot(2), :].astype(BF16)
+                    m1_copy(b, c, side).start()
+
+            @pl.when((t >= 1) & (t < NC + 1))
+            def _():
+                c = t - 1
+                for side in range(2):
+                    m1_copy(b, c, side).wait_recv()
+                    k = 1 if side == 0 else 3
+                    for part in range(2):
+                        q = keep[b, c, part, slot(k), :]
+                        if part == side:
+                            q = q + m1r[b, c, side].astype(F32)
+                        m2s[b, c, side, part] = q.astype(BF16)
+                    m2_copy(b, c, side).start()
+
+            @pl.when(t >= 2)
+            def _():
+                c = t - 2
+                for side in range(2):
+                    m2_copy(b, c, side).wait_recv()
+                for part in range(2):
+                    q = keep[b, c, part, slot(0), :] + m2r[b, c, 0, part].astype(F32) + m2r[b, c, 1, part].astype(F32)
+                    rows = pl.ds(pl.multiple_of(part * 64 + p.x * 16, 16), 16)
+                    for s in range(NS2):
+                        r = rbuf[c, s, b, part, rows, :].astype(F32)
+                        cols = pl.ds(pl.multiple_of(c * CW + s * c2, c2), c2)
+                        at = part * 32 + b * 16
+                        out[at : at + 16, cols] = (r + q[:, s * c2 : (s + 1) * c2]).astype(BF16)
+
+            return 0
+
+        lax.fori_loop(0, NC + 2, one, 0)
+
+    ga = [gather_rows(p, abuf, b, s1, r1, NS1, project(b)) for b in range(2)]
+    gr = [gather_rows(p, rbuf, b, s2, r2, NS2, expand(b)) for b in range(2)]
+    advance(ga[0], 2)
+    advance(ga[1], 1)
+    advance(ga[0], 2)
+    advance(ga[1], 2)
+    advance(ga[0], 3)
+    advance(ga[1], 1)
+    advance(ga[0], 1)
+    advance(ga[1], 4)
+    advance(ga[0], 4)
+    residual(0)
+    advance(gr[0], 3)
+    advance(ga[1], 4)
+    residual(1)
+    advance(gr[0], 1)
+    advance(gr[1], 1)
+    advance(gr[0], 3)
+    advance(gr[1], 2)
+    advance(gr[0], 1)
+    advance(gr[1], 1)
+    advance(gr[0], 2)
+    advance(gr[1], 2)
+    advance(gr[0], 2)
+    activate(0)
+    advance(gr[1], 2)
     wd_copy.wait()
-    lax.fori_loop(0, NC, reduce_down, 0)
-
-    def slot(k):
-        return pl.ds(pl.multiple_of(p.xs[k] * 32, 32), 32)
-
-    def m1_copy(c, side):
-        device = p.right if side == 0 else p.left
-        return remote(m1s.at[c, side], m1r.at[c, side], s3, m1sem.at[side, c], device)
-
-    def m2_copy(c, side):
-        device = p.right if side == 0 else p.left
-        return remote(m2s.at[c, side], m2r.at[c, side], s3, m2sem.at[side, c], device)
-
-    def finish(t, _):
-        @pl.when(t < NC)
-        def _():
-            c = t
-            for side in range(2):
-                z_wait(c, side)
-                keep[c, side] += zr[c, side].astype(F32)
-                m1s[c, side] = keep[c, side, slot(2), :].astype(BF16)
-                m1_copy(c, side).start()
-
-        @pl.when((t >= 1) & (t < NC + 1))
-        def _():
-            c = t - 1
-            for side in range(2):
-                m1_copy(c, side).wait_recv()
-                k = 1 if side == 0 else 3
-                for part in range(2):
-                    q = keep[c, part, slot(k), :]
-                    if part == side:
-                        q = q + m1r[c, side].astype(F32)
-                    m2s[c, side, part] = q.astype(BF16)
-                m2_copy(c, side).start()
-
-        @pl.when(t >= 2)
-        def _():
-            c = t - 2
-            for side in range(2):
-                m2_copy(c, side).wait_recv()
-            for part in range(2):
-                q = keep[c, part, slot(0), :] + m2r[c, 0, part].astype(F32) + m2r[c, 1, part].astype(F32)
-                rows = pl.ds(pl.multiple_of(part * 128 + p.x * 32, 32), 32)
-                for s in range(NS2):
-                    r = rbuf[c, s, part, rows, :].astype(F32)
-                    cols = pl.ds(pl.multiple_of(c * CW + s * c2, c2), c2)
-                    out[part * 32 : (part + 1) * 32, cols] = (r + q[:, s * c2 : (s + 1) * c2]).astype(BF16)
-
-        return 0
-
-    lax.fori_loop(0, NC + 2, finish, 0)
-    pltpu.make_async_copy(zs, zs, s3).wait()
-    pltpu.make_async_copy(m1s, m1s, s3).wait()
-    pltpu.make_async_copy(m2s, m2s, s3).wait()
+    reduce_down(0)
+    advance(gr[1], 4)
+    activate(1)
+    reduce_down(1)
+    finish(0)
+    finish(1)
+    pltpu.make_async_copy(abuf.at[0:7], abuf.at[0:7], s1).wait()
+    pltpu.make_async_copy(rbuf.at[0:7], rbuf.at[0:7], s2).wait()
+    for ref in (zs, m1s, m2s):
+        pltpu.make_async_copy(ref, ref, s3).wait()
 
 
 def layer(q, k, v, hidden, gain, wo, gate, up, down):
@@ -579,33 +645,39 @@
     dma = pltpu.SemaphoreType.DMA
     return pl.pallas_call(
         block_kernel,
-        out_shape=jax.ShapeDtypeStruct((64, 4096), BF16),
-        in_specs=[vmem, vmem, vmem, vmem, vmem, hbm, hbm, hbm, hbm],
+        out_shape=pltpu.VMEM((64, 4096), BF16),
+        in_specs=[hbm] * 9,
         out_specs=vmem,
         scratch_shapes=[
+            pltpu.VMEM((64, 2048), BF16),
+            pltpu.VMEM((64, 1024), BF16),
+            pltpu.VMEM((64, 1024), BF16),
+            pltpu.VMEM((64, 4096), BF16),
+            pltpu.VMEM((32, 128), F32),
             pltpu.VMEM((16, 512, 384), BF16),
             pltpu.VMEM((512, 256), BF16),
             pltpu.VMEM((1024, 128), BF16),
             pltpu.VMEM((1024, 256), F32),
             pltpu.VMEM((1024, 128), F32),
-            pltpu.VMEM((8, NS1, 2, 256, 256 // NS1), BF16),
-            pltpu.VMEM((8, NS2, 2, 256, 512 // NS2), BF16),
+            pltpu.VMEM((8, NS1, 2, 2, 128, 256 // NS1), BF16),
+            pltpu.VMEM((8, NS2, 2, 2, 128, 512 // NS2), BF16),
             pltpu.VMEM((512, 512), BF16),
             pltpu.VMEM((8, 2, 128, 512), BF16),
             pltpu.VMEM((4096, 2 * FFL), BF16),
             pltpu.VMEM((FFL, 4096), BF16),
             pltpu.VMEM((512, 512), F32),
             pltpu.VMEM((512, 2 * FFL), F32),
-            pltpu.VMEM((512, 512), BF16),
+            pltpu.VMEM((2, 256, 512), BF16),
             pltpu.VMEM((512, 128), F32),
             pltpu.VMEM((512, FFL), BF16),
-            pltpu.VMEM((NC, 2, 128, CW), BF16),
-            pltpu.VMEM((NC, 2, 128, CW), BF16),
-            pltpu.VMEM((NC, 2, 128, CW), F32),
-            pltpu.VMEM((NC, 2, 32, CW), BF16),
-            pltpu.VMEM((NC, 2, 32, CW), BF16),
-            pltpu.VMEM((NC, 2, 2, 32, CW), BF16),
-            pltpu.VMEM((NC, 2, 2, 32, CW), BF16),
+            pltpu.VMEM((2, NC, 2, 64, CW), BF16),
+            pltpu.VMEM((2, NC, 2, 64, CW), BF16),
+            pltpu.VMEM((2, NC, 2, 64, CW), F32),
+            pltpu.VMEM((2, NC, 2, 16, CW), BF16),
+            pltpu.VMEM((2, NC, 2, 16, CW), BF16),
+            pltpu.VMEM((2, NC, 2, 2, 16, CW), BF16),
+            pltpu.VMEM((2, NC, 2, 2, 16, CW), BF16),
+            dma((5,)),
             dma((18,)),
             dma,
             dma((2,)),
@@ -617,13 +689,13 @@
             dma((2,)),
             dma((8,)),
             dma,
-            dma((14, NS1)),
+            dma((14, NS1, 2)),
             dma,
-            dma((14, NS2)),
+            dma((14, NS2, 2)),
             dma,
-            dma((2, NC)),
-            dma((2, NC)),
-            dma((2, NC)),
+            dma((2, 2, NC)),
+            dma((2, 2, NC)),
+            dma((2, 2, NC)),
         ],
         compiler_params=pltpu.CompilerParams(
             collective_id=1, has_side_effects=True, vmem_limit_bytes=62 * 1024 * 1024

time: 122 us -> 133 us (1.090)
  Pallas kernels: 120 us -> 132 us
    pallas_call x1, Pallas kernels: 120 us -> 132 us  [layer(): pl.pallas_call(block_kernel, out_shape=pltpu.VMEM((64, 4096), BF16), in_s...]
where the time goes in v4:
time: 133 us
  Pallas kernels  132 us (99%)
    pallas_call x1, Pallas kernels, layer(): pl.pallas_call(block_kernel, out_shape=pltpu.VMEM((64, 4096), BF16), in_s...  132 us

profile of v4, /device:TPU:24, one launch (start us, length us, event | category | flops | bytes accessed | tf_op | source)
XLA Modules:
  0.0 132.7 jit_solution(18146860551259453787)
XLA Ops:
  0.0 131.9 %layer.1 = bf16[64,4096]{1,0:T(8,128)(2,1)S(1)} custom-call(bf16[64,2048]{1,0:T(8,128)(2,1)} %q_hbm.1, bf16[64,1024]{1,0:T(8,128)(2,1)} %k_hbm.1, bf16[64,1024]{1,0:T(8,128)(2,1)} %v_hbm.1, bf16[64,4096]{1,0:T(8,128)(2,1)} %hid_hbm.1, f32[32,128]{1,0:T(8,128)} %bitcast.1, bf16[256,4096]{1,0:T(8,128)(2,1)} %wo_hbm.1, bf16[4096,896]{1,0:T(8,128)(2,1)} %gate_hbm.1, ...), custom_call_target="tpu_custom_call" | custom-call | flops 16499999744 | bytes 24000000 | tf_op jit(solution)/shard_map/layer/pallas_call | solution.py:646
  131.9 0.8 copy.11

commit v5 on v4

--- a/solution.py
+++ b/solution.py
@@ -67,7 +67,7 @@
     )
 
 
-def gather_rows(p, buf, batch, send_sem, recv, steps, compute):
+def gather_rows(p, buf, batch, send_sem, recv, steps, compute, across_first=()):
     def send(h, s, half, to_half, kind, device):
         src, dst = buf.at[h, s, batch, half], buf.at[h, s, batch, to_half]
         remote(src, dst, send_sem, recv.at[kind, s, batch], device).start()
@@ -77,53 +77,78 @@
         remote(ref, ref, send_sem, recv.at[kind, s, batch], p.right).wait_recv()
 
     me, left, right, far = p.here(0), p.here(3), p.here(1), p.here(2)
+    twin, twin_left, twin_right, twin_far = p.other(0), p.other(3), p.other(1), p.other(2)
+    along_first = [s for s in range(steps) if s not in across_first]
     for s in range(steps):
         send(me, s, 0, 0, 0, p.right)
         send(me, s, 1, 1, 4, p.left)
         send(me, s, 0, 1, 6, p.above)
         send(me, s, 1, 0, 10, p.below)
     yield
+    compute(me, True)
+    yield
+    for s in range(steps):
+        wait(left, s, 0, 0)
+        send(left, s, 0, 0, 2, p.right)
+        wait(right, s, 1, 4)
+        send(right, s, 1, 1, 5, p.left)
+        if s in along_first:
+            send(left, s, 0, 1, 7, p.above)
+            send(right, s, 1, 0, 12, p.below)
+    yield
     for s in range(steps):
         send(me, s, 1, 1, 1, p.right)
         send(me, s, 0, 0, 3, p.left)
     yield
-    compute(me, True)
-    yield
-    for s in range(steps):
-        wait(left, s, 0, 0)
-        send(left, s, 0, 0, 2, p.right)
-        send(left, s, 0, 1, 7, p.above)
-        wait(right, s, 1, 4)
-        send(right, s, 1, 1, 5, p.left)
-        send(right, s, 1, 0, 12, p.below)
-    yield
-    for s in range(steps):
-        wait(p.other(0), s, 1, 6)
-        wait(p.other(0), s, 0, 10)
-    compute(p.other(0), False)
+    for s in range(steps):
+        wait(twin, s, 1, 6)
+        wait(twin, s, 0, 10)
+        if s in across_first:
+            send(twin, s, 0, 0, 11, p.right)
+            send(twin, s, 1, 1, 8, p.left)
+            send(twin, s, 1, 1, 7, p.right)
+            send(twin, s, 0, 0, 12, p.left)
+    compute(twin, False)
+    yield
+    for s in range(steps):
+        wait(far, s, 0, 2)
+        wait(far, s, 1, 5)
+        if s in along_first:
+            send(far, s, 0, 1, 9, p.above)
+            send(far, s, 1, 0, 13, p.below)
     yield
     for s in range(steps):
         wait(left, s, 1, 1)
-        send(left, s, 1, 0, 11, p.below)
         wait(right, s, 0, 3)
-        send(right, s, 0, 1, 8, p.above)
+        if s in along_first:
+            send(left, s, 1, 0, 11, p.below)
+            send(right, s, 0, 1, 8, p.above)
+    for s in across_first:
+        wait(twin_left, s, 0, 11)
+        send(twin_left, s, 0, 0, 13, p.right)
+        wait(twin_right, s, 1, 8)
+        send(twin_right, s, 1, 1, 9, p.left)
     yield
     compute(left, False)
     compute(right, False)
-    yield
-    for s in range(steps):
-        wait(far, s, 0, 2)
-        send(far, s, 0, 1, 9, p.above)
-        wait(far, s, 1, 5)
-        send(far, s, 1, 0, 13, p.below)
-    yield
     compute(far, False)
-    for k, up, down in ((3, 7, 11), (1, 8, 12), (2, 9, 13)):
-        yield
-        for s in range(steps):
-            wait(p.other(k), s, 1, up)
-            wait(p.other(k), s, 0, down)
-        compute(p.other(k), False)
+    yield
+    for s in range(steps):
+        wait(twin_left, s, 1, 7)
+        if s in along_first:
+            wait(twin_left, s, 0, 11)
+    compute(twin_left, False)
+    yield
+    for s in range(steps):
+        wait(twin_right, s, 0, 12)
+        if s in along_first:
+            wait(twin_right, s, 1, 8)
+    compute(twin_right, False)
+    yield
+    for s in range(steps):
+        wait(twin_far, s, 1, 9)
+        wait(twin_far, s, 0, 13)
+    compute(twin_far, False)
 
 
 def advance(stages, count):
@@ -195,13 +220,6 @@
     def wait_shared(dz, kk, sem):
         ref = kv.at[block(dz, kk, True), :, 0:256]
         remote(ref, ref, sk, sem, p.partner).wait_recv()
-
-    def send_both(dz):
-        i = 3 * dz
-        send_piece(dz, 0, 0, ysem.at[0, i], p.up)
-        send_piece(dz, 0, 1, ysem.at[1, i + 1], p.down)
-        send_piece(dz, 0, 1, ysem.at[0, i + 1], p.up)
-        send_piece(dz, 0, 0, ysem.at[1, i], p.down)
 
     def forward(dz):
         i = 3 * dz
@@ -324,10 +342,12 @@
         absorb_b(p.chip, False)
 
     forward(0)
+    for part in (p.zl, 1 - p.zl):
+        ref = kv.at[block(1, 0), pl.ds(pl.multiple_of(part * 256, 256), 256), 0:256]
+        remote(ref, ref, sk, zrecv.at[part], p.up).wait_recv()
+        remote(ref, ref, sk, ysem.at[0, 3 + part], p.up).start()
+        remote(ref, ref, sk, ysem.at[1, 3 + part], p.down).start()
     near_done(0)
-    for part in range(2):
-        wait_piece(1, 0, part, zrecv.at[part])
-    send_both(1)
     share(1, 0, csem.at[4])
     half = pl.ds(pl.multiple_of(p.core * 128, 128), 128)
     for kx in range(4):
@@ -406,6 +426,8 @@
 NS1 = 1
 NS2 = 2
 NC = 8
+LAG = 5
+ACROSS_FIRST = ((), ())
 CW = 512
 FFL = 896
 
@@ -536,12 +558,13 @@
         def one(c, _):
             cols = pl.ds(pl.multiple_of(c * CW, CW), CW)
             part = jnp.dot(inner[b * 256 : (b + 1) * 256], wd[:, cols], preferred_element_type=F32)
-            keep[b, c, 0] = part[0:64]
-            zs[b, c, 0] = part[64:128].astype(BF16)
-            zs[b, c, 1] = part[128:192].astype(BF16)
-            keep[b, c, 1] = part[192:256]
-            remote(zs.at[b, c, 0], zr.at[b, c, 1], s3, zsem.at[b, 1, c], p.above).start()
-            remote(zs.at[b, c, 1], zr.at[b, c, 0], s3, zsem.at[b, 0, c], p.below).start()
+            n = b * NC + c
+            keep[n, 0] = part[0:64]
+            zs[n, 0] = part[64:128].astype(BF16)
+            zs[n, 1] = part[128:192].astype(BF16)
+            keep[n, 1] = part[192:256]
+            remote(zs.at[n, 0], zr.at[n, 1], s3, zsem.at[1, n], p.above).start()
+            remote(zs.at[n, 1], zr.at[n, 0], s3, zsem.at[0, n], p.below).start()
             return 0
 
         lax.fori_loop(0, NC, one, 0)
@@ -549,90 +572,92 @@
     def slot(k):
         return pl.ds(pl.multiple_of(p.xs[k] * 16, 16), 16)
 
-    def m1_copy(b, c, side):
+    def m1_copy(n, side):
         device = p.right if side == 0 else p.left
-        return remote(m1s.at[b, c, side], m1r.at[b, c, side], s3, m1sem.at[b, side, c], device)
-
-    def m2_copy(b, c, side):
+        return remote(m1s.at[n, side], m1r.at[n, side], s3, m1sem.at[side, n], device)
+
+    def m2_copy(n, side):
         device = p.right if side == 0 else p.left
-        return remote(m2s.at[b, c, side], m2r.at[b, c, side], s3, m2sem.at[b, side, c], device)
-
-    def finish(b):
+        return remote(m2s.at[n, side], m2r.at[n, side], s3, m2sem.at[side, n], device)
+
+    def finish():
         def one(t, _):
-            @pl.when(t < NC)
+            @pl.when(t < 2 * NC)
             def _():
-                c = t
+                n = t
                 for side in range(2):
-                    ref = zr.at[b, c, side]
-                    remote(ref, ref, s3, zsem.at[b, side, c], p.right).wait_recv()
-                    keep[b, c, side] += zr[b, c, side].astype(F32)
-                    m1s[b, c, side] = keep[b, c, side, slot(2), :].astype(BF16)
-                    m1_copy(b, c, side).start()
-
-            @pl.when((t >= 1) & (t < NC + 1))
+                    ref = zr.at[n, side]
+                    remote(ref, ref, s3, zsem.at[side, n], p.right).wait_recv()
+                    keep[n, side] += zr[n, side].astype(F32)
+                    m1s[n, side] = keep[n, side, slot(2), :].astype(BF16)
+                    m1_copy(n, side).start()
+
+            @pl.when((t >= LAG) & (t < 2 * NC + LAG))
             def _():
-                c = t - 1
+                n = t - LAG
                 for side in range(2):
-                    m1_copy(b, c, side).wait_recv()
+                    m1_copy(n, side).wait_recv()
                     k = 1 if side == 0 else 3
                     for part in range(2):
-                        q = keep[b, c, part, slot(k), :]
+                        q = keep[n, part, slot(k), :]
                         if part == side:
-                            q = q + m1r[b, c, side].astype(F32)
-                        m2s[b, c, side, part] = q.astype(BF16)
-                    m2_copy(b, c, side).start()
-
-            @pl.when(t >= 2)
+                            q = q + m1r[n, side].astype(F32)
+                        m2s[n, side, part] = q.astype(BF16)
+                    m2_copy(n, side).start()
+
+            @pl.when(t >= 2 * LAG)
             def _():
-                c = t - 2
+                n = t - 2 * LAG
+                b, c = n // NC, lax.rem(n, NC)
                 for side in range(2):
-                    m2_copy(b, c, side).wait_recv()
+                    m2_copy(n, side).wait_recv()
                 for part in range(2):
-                    q = keep[b, c, part, slot(0), :] + m2r[b, c, 0, part].astype(F32) + m2r[b, c, 1, part].astype(F32)
+                    q = keep[n, part, slot(0), :] + m2r[n, 0, part].astype(F32) + m2r[n, 1, part].astype(F32)
                     rows = pl.ds(pl.multiple_of(part * 64 + p.x * 16, 16), 16)
                     for s in range(NS2):
                         r = rbuf[c, s, b, part, rows, :].astype(F32)
                         cols = pl.ds(pl.multiple_of(c * CW + s * c2, c2), c2)
-                        at = part * 32 + b * 16
-                        out[at : at + 16, cols] = (r + q[:, s * c2 : (s + 1) * c2]).astype(BF16)
+                        to = pl.ds(pl.multiple_of(part * 32 + b * 16, 16), 16)
+                        out[to, cols] = (r + q[:, s * c2 : (s + 1) * c2]).astype(BF16)
 
             return 0
 
-        lax.fori_loop(0, NC + 2, one, 0)
+        lax.fori_loop(0, 2 * NC + 2 * LAG, one, 0)
 
     ga = [gather_rows(p, abuf, b, s1, r1, NS1, project(b)) for b in range(2)]
-    gr = [gather_rows(p, rbuf, b, s2, r2, NS2, expand(b)) for b in range(2)]
-    advance(ga[0], 2)
-    advance(ga[1], 1)
-    advance(ga[0], 2)
-    advance(ga[1], 2)
-    advance(ga[0], 3)
+    gr = [gather_rows(p, rbuf, b, s2, r2, NS2, expand(b), ACROSS_FIRST[b]) for b in range(2)]
+    advance(ga[0], 1)
     advance(ga[1], 1)
     advance(ga[0], 1)
-    advance(ga[1], 4)
+    advance(ga[1], 1)
+    advance(ga[0], 1)
+    advance(ga[1], 1)
+    advance(ga[0], 1)
+    advance(ga[1], 1)
+    advance(ga[0], 1)
+    advance(ga[1], 1)
+    advance(ga[0], 1)
+    advance(ga[1], 1)
+    advance(ga[0], 1)
+    advance(ga[1], 1)
     advance(ga[0], 4)
     residual(0)
-    advance(gr[0], 3)
+    advance(gr[0], 2)
     advance(ga[1], 4)
     residual(1)
+    advance(gr[0], 5)
+    advance(gr[1], 1)
     advance(gr[0], 1)
-    advance(gr[1], 1)
+    advance(gr[1], 3)
     advance(gr[0], 3)
-    advance(gr[1], 2)
-    advance(gr[0], 1)
-    advance(gr[1], 1)
-    advance(gr[0], 2)
-    advance(gr[1], 2)
-    advance(gr[0], 2)
     activate(0)
-    advance(gr[1], 2)
     wd_copy.wait()
+    advance(gr[1], 3)
     reduce_down(0)
     advance(gr[1], 4)
     activate(1)
     reduce_down(1)
-    finish(0)
-    finish(1)
+    finish()
     pltpu.make_async_copy(abuf.at[0:7], abuf.at[0:7], s1).wait()
     pltpu.make_async_copy(rbuf.at[0:7], rbuf.at[0:7], s2).wait()
     for ref in (zs, m1s, m2s):
@@ -670,13 +695,13 @@
             pltpu.VMEM((2, 256, 512), BF16),
             pltpu.VMEM((512, 128), F32),
             pltpu.VMEM((512, FFL), BF16),
-            pltpu.VMEM((2, NC, 2, 64, CW), BF16),
-            pltpu.VMEM((2, NC, 2, 64, CW), BF16),
-            pltpu.VMEM((2, NC, 2, 64, CW), F32),
-            pltpu.VMEM((2, NC, 2, 16, CW), BF16),
-            pltpu.VMEM((2, NC, 2, 16, CW), BF16),
-            pltpu.VMEM((2, NC, 2, 2, 16, CW), BF16),
-            pltpu.VMEM((2, NC, 2, 2, 16, CW), BF16),
+            pltpu.VMEM((2 * NC, 2, 64, CW), BF16),
+            pltpu.VMEM((2 * NC, 2, 64, CW), BF16),
+            pltpu.VMEM((2 * NC, 2, 64, CW), F32),
+            pltpu.VMEM((2 * NC, 2, 16, CW), BF16),
+            pltpu.VMEM((2 * NC, 2, 16, CW), BF16),
+            pltpu.VMEM((2 * NC, 2, 2, 16, CW), BF16),
+            pltpu.VMEM((2 * NC, 2, 2, 16, CW), BF16),
             dma((5,)),
             dma((18,)),
             dma,
@@ -693,9 +718,9 @@
             dma,
             dma((14, NS2, 2)),
             dma,
-            dma((2, 2, NC)),
-            dma((2, 2, NC)),
-            dma((2, 2, NC)),
+            dma((2, 2 * NC)),
+            dma((2, 2 * NC)),
+            dma((2, 2 * NC)),
         ],
         compiler_params=pltpu.CompilerParams(
             collective_id=1, has_side_effects=True, vmem_limit_bytes=62 * 1024 * 1024

time: 133 us -> 116 us (0.87)
  Pallas kernels: 132 us -> 115 us
    pallas_call x1, Pallas kernels: 132 us -> 115 us  [layer(): pl.pallas_call(block_kernel, out_shape=pltpu.VMEM((64, 4096), BF16), in_s...]
where the time goes in v5:
time: 116 us
  Pallas kernels  115 us (99%)
    pallas_call x1, Pallas kernels, layer(): pl.pallas_call(block_kernel, out_shape=pltpu.VMEM((64, 4096), BF16), in_s...  115 us

profile of v5, /device:TPU:24, one launch (start us, length us, event | category | flops | bytes accessed | tf_op | source)
XLA Modules:
  0.0 115.5 jit_solution(10947889326506672613)
XLA Ops:
  0.0 114.7 %layer.1 = bf16[64,4096]{1,0:T(8,128)(2,1)S(1)} custom-call(bf16[64,2048]{1,0:T(8,128)(2,1)} %q_hbm.1, bf16[64,1024]{1,0:T(8,128)(2,1)} %k_hbm.1, bf16[64,1024]{1,0:T(8,128)(2,1)} %v_hbm.1, bf16[64,4096]{1,0:T(8,128)(2,1)} %hid_hbm.1, f32[32,128]{1,0:T(8,128)} %bitcast.1, bf16[256,4096]{1,0:T(8,128)(2,1)} %wo_hbm.1, bf16[4096,896]{1,0:T(8,128)(2,1)} %gate_hbm.1, ...), custom_call_target="tpu_custom_call" | custom-call | flops 16499999744 | bytes 24000000 | tf_op jit(solution)/shard_map/layer/pallas_call | solution.py:671
  114.7 0.8 copy.11

commit v6 on v5

--- a/solution.py
+++ b/solution.py
@@ -123,6 +123,7 @@
         if s in along_first:
             send(left, s, 1, 0, 11, p.below)
             send(right, s, 0, 1, 8, p.above)
+    yield
     for s in across_first:
         wait(twin_left, s, 0, 11)
         send(twin_left, s, 0, 0, 13, p.right)
@@ -367,12 +368,15 @@
     wait_shared(0, 1, csem.at[1])
 
     def near_step(t, _):
+        @pl.when(t == 1)
+        def _():
+            forward(1)
+
         seen(p.chip_at(0, 3 - 2 * t))
         return 0
 
     lax.fori_loop(0, 2, near_step, 0)
     far_done(0)
-    forward(1)
     wait_shared(1, 0, csem.at[4])
     chip = p.chip_at(1, 0)
 
@@ -381,12 +385,22 @@
         absorb_a(chip, False)
 
     absorb_b(chip, True)
-    near_done(1)
-    wait_shared(0, 2, csem.at[2])
-    wait_shared(1, 3, csem.at[7])
-    wait_shared(1, 1, csem.at[5])
 
     def late_step(t, _):
+        @pl.when(t == 0)
+        def _():
+            wait_shared(0, 2, csem.at[2])
+
+        @pl.when(t == 1)
+        def _():
+            near_done(1)
+            wait_shared(1, 3, csem.at[7])
+
+        @pl.when(t == 2)
+        def _():
+            far_done(1)
+            wait_shared(1, 1, csem.at[5])
+
         @pl.when(t == 3)
         def _():
             wown.wait()
@@ -394,7 +408,6 @@
             remote(ref, ref, sk, w1, p.up).wait_recv()
             ref = wo.at[:, p.core]
             remote(ref, ref, sk, w2, p.partner).start()
-            far_done(1)
             wait_shared(1, 2, csem.at[6])
 
         seen(p.chip_at(jnp.minimum(t, 1), 2 + t - 3 * (t // 2)))
@@ -427,7 +440,7 @@
 NS2 = 2
 NC = 8
 LAG = 5
-ACROSS_FIRST = ((), ())
+ACROSS_FIRST = ((), (1,))
 CW = 512
 FFL = 896
 
@@ -554,7 +567,7 @@
 
         lax.fori_loop(0, 7, tile, 0)
 
-    def reduce_down(b):
+    def reduce_down(b, start, stop):
         def one(c, _):
             cols = pl.ds(pl.multiple_of(c * CW, CW), CW)
             part = jnp.dot(inner[b * 256 : (b + 1) * 256], wd[:, cols], preferred_element_type=F32)
@@ -567,7 +580,7 @@
             remote(zs.at[n, 1], zr.at[n, 0], s3, zsem.at[0, n], p.below).start()
             return 0
 
-        lax.fori_loop(0, NC, one, 0)
+        lax.fori_loop(start, stop, one, 0)
 
     def slot(k):
         return pl.ds(pl.multiple_of(p.xs[k] * 16, 16), 16)
@@ -640,23 +653,25 @@
     advance(ga[1], 1)
     advance(ga[0], 1)
     advance(ga[1], 1)
-    advance(ga[0], 4)
+    advance(ga[0], 5)
     residual(0)
     advance(gr[0], 2)
-    advance(ga[1], 4)
+    advance(ga[1], 5)
     residual(1)
     advance(gr[0], 5)
     advance(gr[1], 1)
-    advance(gr[0], 1)
+    advance(gr[0], 2)
     advance(gr[1], 3)
     advance(gr[0], 3)
     activate(0)
     wd_copy.wait()
     advance(gr[1], 3)
-    reduce_down(0)
+    reduce_down(0, 0, 3)
+    advance(gr[1], 1)
+    reduce_down(0, 3, NC)
     advance(gr[1], 4)
     activate(1)
-    reduce_down(1)
+    reduce_down(1, 0, NC)
     finish()
     pltpu.make_async_copy(abuf.at[0:7], abuf.at[0:7], s1).wait()
     pltpu.make_async_copy(rbuf.at[0:7], rbuf.at[0:7], s2).wait()

time: 116 us -> 113 us (0.974)
  Pallas kernels: 115 us -> 112 us
    pallas_call x1, Pallas kernels: 115 us -> 112 us  [layer(): pl.pallas_call(block_kernel, out_shape=pltpu.VMEM((64, 4096), BF16), in_s...]
where the time goes in v6:
time: 113 us
  Pallas kernels  112 us (99%)
    pallas_call x1, Pallas kernels, layer(): pl.pallas_call(block_kernel, out_shape=pltpu.VMEM((64, 4096), BF16), in_s...  112 us

profile of v6, /device:TPU:24, one launch (start us, length us, event | category | flops | bytes accessed | tf_op | source)
XLA Modules:
  0.0 112.7 jit_solution(11124088943542487775)
XLA Ops:
  0.0 111.9 %layer.1 = bf16[64,4096]{1,0:T(8,128)(2,1)S(1)} custom-call(bf16[64,2048]{1,0:T(8,128)(2,1)} %q_hbm.1, bf16[64,1024]{1,0:T(8,128)(2,1)} %k_hbm.1, bf16[64,1024]{1,0:T(8,128)(2,1)} %v_hbm.1, bf16[64,4096]{1,0:T(8,128)(2,1)} %hid_hbm.1, f32[32,128]{1,0:T(8,128)} %bitcast.1, bf16[256,4096]{1,0:T(8,128)(2,1)} %wo_hbm.1, bf16[4096,896]{1,0:T(8,128)(2,1)} %gate_hbm.1, ...), custom_call_target="tpu_custom_call" | custom-call | flops 16499999744 | bytes 24000000 | tf_op jit(solution)/shard_map/layer/pallas_call | solution.py:686
  111.9 0.8 copy.11

commit v7 on v6

--- a/solution.py
+++ b/solution.py
@@ -420,10 +420,10 @@
         a = (oa[r * 384 : (r + 1) * 384, 0:128] / oa[r * 384 : (r + 1) * 384, 128:256]).astype(BF16)
         o = (oa[768 + r * 128 : 896 + r * 128, 0:128] / oa[768 + r * 128 : 896 + r * 128, 128:256]).astype(BF16)
         for b in range(2):
-            abuf[p.head, 0, b, 0, 0:64, cols] = batch_rows(a[0:128], b)
-            abuf[p.head, 0, b, p.zl, pl.ds(pl.multiple_of((1 - p.zl) * 64, 64), 64), cols] = batch_rows(a[128:256], b)
-            abuf[p.head, 0, b, 1, 64:128, cols] = batch_rows(a[256:384], b)
-            abuf[p.head, 0, b, 1 - p.zl, pl.ds(pl.multiple_of(p.zl * 64, 64), 64), cols] = batch_rows(o, b)
+            abuf[p.head, r, b, 0, 0:64, :] = batch_rows(a[0:128], b)
+            abuf[p.head, r, b, p.zl, pl.ds(pl.multiple_of((1 - p.zl) * 64, 64), 64), :] = batch_rows(a[128:256], b)
+            abuf[p.head, r, b, 1, 64:128, :] = batch_rows(a[256:384], b)
+            abuf[p.head, r, b, 1 - p.zl, pl.ds(pl.multiple_of(p.zl * 64, 64), 64), :] = batch_rows(o, b)
 
     ref = hid.at[0:448]
     remote(ref, ref, sk, h1, p.up).wait_recv()
@@ -436,7 +436,7 @@
         pltpu.make_async_copy(ref, ref, sk).wait()
 
 
-NS1 = 1
+NS1 = 2
 NS2 = 2
 NC = 8
 LAG = 5
@@ -511,7 +511,8 @@
         rows = slice(b * 256, (b + 1) * 256)
 
         def add(h, first):
-            part = jnp.dot(abuf[h, 0, b].reshape(256, 256), wo[h].reshape(256, 512), preferred_element_type=F32)
+            a = jnp.concatenate([abuf[h, s, b].reshape(256, 256 // NS1) for s in range(NS1)], axis=1)
+            part = jnp.dot(a, wo[h].reshape(256, 512), preferred_element_type=F32)
             if first:
                 held = jnp.concatenate([batch_rows(hid[g * 128 : (g + 1) * 128], b) for g in range(4)], axis=0)
                 oacc[rows] = held.astype(F32) + part

time: 113 us -> 112 us (level)
  no operation moved by 1% of the time
where the time goes in v7:
time: 112 us
  Pallas kernels  111 us (99%)
    pallas_call x1, Pallas kernels, layer(): pl.pallas_call(block_kernel, out_shape=pltpu.VMEM((64, 4096), BF16), in_s...  111 us

profile of v7, /device:TPU:24, one launch (start us, length us, event | category | flops | bytes accessed | tf_op | source)
XLA Modules:
  0.0 111.9 jit_solution(17352968763781944707)
XLA Ops:
  0.0 111.1 %layer.1 = bf16[64,4096]{1,0:T(8,128)(2,1)S(1)} custom-call(bf16[64,2048]{1,0:T(8,128)(2,1)} %q_hbm.1, bf16[64,1024]{1,0:T(8,128)(2,1)} %k_hbm.1, bf16[64,1024]{1,0:T(8,128)(2,1)} %v_hbm.1, bf16[64,4096]{1,0:T(8,128)(2,1)} %hid_hbm.1, f32[32,128]{1,0:T(8,128)} %bitcast.1, bf16[256,4096]{1,0:T(8,128)(2,1)} %wo_hbm.1, bf16[4096,896]{1,0:T(8,128)(2,1)} %gate_hbm.1, ...), custom_call_target="tpu_custom_call" | custom-call | flops 16499999744 | bytes 24000000 | tf_op jit(solution)/shard_map/layer/pallas_call | solution.py:687
  111.1 0.8 copy.11
